TPU v7x, 128 devices: a whole 4x4x4 slice. The times are simulated.
128 devices in a mesh: data: 1, node: 2 (over core), expert: 64 (over z, y, x).
Axes of the slice: x: 4, y: 4, z: 4, core: 2. Of those that a mesh axis runs over, the one named last changes fastest.
Arguments:
- tokens: bfloat16 [32768, 2048], P(('data', 'node', 'expert'))
- expert_ids: int32 [32768, 8], P(('data', 'node', 'expert'))
- gate_weights: float32 [32768, 8], P(('data', 'node', 'expert'))
- slot_ids: int32 [32768, 8], P(('data', 'node', 'expert'))
- w_gate: bfloat16 [128, 2048, 768], P(('node', 'expert'))
- w_up: bfloat16 [128, 2048, 768], P(('node', 'expert'))
- w_down: bfloat16 [128, 768, 2048], P(('node', 'expert'))
Outputs:
- output: bfloat16 [32768, 2048], P(('data', 'node', 'expert'))
All inputs are finite; a program needn't handle non-finite values.
Results may differ from a plain program's by a relative error of at most 0.00153.
Values are sent between devices in bfloat16 or wider.
A program may use at most 1 GiB of HBM per device.

v0:
```python
import jax
import jax.numpy as jnp
from jax import lax
from jax.sharding import PartitionSpec as P

CAP_FACTOR = 2


def capacity(rows, top_k, experts):
    return ((CAP_FACTOR * rows * top_k + 8 * experts - 1) // (8 * experts)) * 8


def solution(mesh):
    group_axes = ("node", "expert")
    group_size = mesh.shape["node"] * mesh.shape["expert"]
    tok_spec = P(("data", "node", "expert"), None)
    weight_spec = P(("node", "expert"), None, None)

    def local_layer(tokens, expert_ids, gate_weights, slot_ids, w_gate, w_up, w_down):
        rows, width = tokens.shape
        top_k = expert_ids.shape[1]
        local_experts = w_gate.shape[0]
        experts = local_experts * group_size
        slot_count = capacity(rows, top_k, experts)
        flat_pos = jnp.where(slot_ids >= 0, expert_ids * slot_count + slot_ids, experts * slot_count)
        tok_index = jnp.broadcast_to(jnp.arange(rows, dtype=jnp.int32)[:, None], (rows, top_k))
        src_table = jnp.full((experts * slot_count,), rows, jnp.int32).at[flat_pos.reshape(-1)].set(tok_index.reshape(-1), mode="drop")
        send_buf = jnp.take(tokens, src_table, axis=0, mode="fill", fill_value=0)
        send_buf = send_buf.reshape(group_size, local_experts, 1, slot_count, width)
        recv_buf = lax.all_to_all(send_buf, group_axes, 0, 2, tiled=True)
        recv_buf = recv_buf.reshape(local_experts, group_size * slot_count, width)
        proj_gate = jnp.einsum("erd,edf->erf", recv_buf, w_gate, preferred_element_type=jnp.float32)
        proj_up = jnp.einsum("erd,edf->erf", recv_buf, w_up, preferred_element_type=jnp.float32)
        hidden = (jax.nn.silu(proj_gate) * proj_up).astype(jnp.bfloat16)
        expert_out = jnp.einsum("erf,efd->erd", hidden, w_down, preferred_element_type=jnp.float32).astype(jnp.bfloat16)
        expert_out = expert_out.reshape(local_experts, group_size, slot_count, width)
        returned = lax.all_to_all(expert_out, group_axes, 1, 0, tiled=True)
        returned = returned.reshape(experts * slot_count, width)
        picked = jnp.take(returned, flat_pos, axis=0, mode="fill", fill_value=0)
        combined = jnp.sum(gate_weights[:, :, None] * picked.astype(jnp.float32), axis=1)
        return combined.astype(jnp.bfloat16)

    return jax.shard_map(local_layer, mesh=mesh, in_specs=(tok_spec, tok_spec, tok_spec, tok_spec, weight_spec, weight_spec, weight_spec), out_specs=tok_spec, check_vma=False)
```

profile of v0, /device:TPU:39, one launch (start us, length us, event | category | flops | bytes accessed | tf_op | source)
XLA Modules:
  0.0 684.2 jit_solution(6818801884356223916)
XLA Ops:
  0.0 0.0 copy-start
  0.0 1.5 compare_and_fusion.1
  1.5 0.0 copy-start.3
  1.5 0.1 copy.16
  1.6 0.1 reshape.107
  1.7 0.1 reshape.135
  1.9 8.1 %scatter_custom_fusion = s32[4096]{0:T(1024)S(1)} fusion(s32[2048]{0:T(1024)S(1)} %bitcast.29, s32[2048]{0:T(1024)S(1)} %reshape.135, s32[]{:T(128)} %constant.24.clone.1), kind=kCustom, calls=%fused_computation.17 | custom fusion | bytes 16388 | tf_op jit(solution)/shard_map/scatter | solution.py:27
  10.0 0.1 broadcast_in_dim.45
  10.0 32.7 %gather_fusion = bf16[4096,2048]{1,0:T(8,128)(2,1)} fusion(bf16[256,2048]{1,0:T(8,128)(2,1)} %param.7, s32[4096]{0:T(1024)S(1)} %fusion.5), kind=kCustom, calls=%fused_computation | custom fusion | bytes 33570816 | tf_op jit(solution)/shard_map/jit(_take)/gather | solution.py:28
  42.8 0.0 copy-done.3
  42.8 8.3 %broadcast_select_fusion = bf16[128,1,1,32,2048]{4,3,2,1,0:T(8,128)(2,1)S(1)} fusion(bf16[128,1,1,32,2048]{4,3,2,1,0:T(8,128)(2,1)} %bitcast.25, pred[128,32]{1,0:T(8,128)(4,1)S(1)} %broadcast_in_dim.45), kind=kLoop, calls=%fused_computation.4 | loop fusion | flops 8388608 | bytes 33558528 | tf_op jit(solution)/shard_map/jit(_take)/select_n | solution.py:28
  51.0 0.0 copy-start.7
  51.1 242.6 %all_to_all.8 = bf16[128,1,1,32,2048]{4,3,2,1,0:T(8,128)(2,1)S(1)} all-to-all(bf16[128,1,1,32,2048]{4,3,2,1,0:T(8,128)(2,1)S(1)} %broadcast_select_fusion), channel_id=1, replica_groups=mesh['data'=1,'node'=2,'expert'=64] {'node','expert'}, dimensions={0} | all-to-all | bytes 33554432 | tf_op jit(solution)/shard_map/all_to_all | solution.py:30
  293.6 0.0 copy-start.2
  293.6 5.7 copy-done.2
  299.4 0.0 copy-done.7
  299.4 16.2 %fusion.3 = f32[4096,768]{1,0:T(8,128)} fusion(bf16[4096,2048]{1,0:T(8,128)(2,1)S(1)} %bitcast.27, bf16[1,2048,768]{2,1,0:T(8,128)(2,1)S(1)} %copy-done.7), kind=kOutput, calls=%fused_computation.10 | convolution fusion | flops 12884901888 | bytes 32505856 | tf_op jit(solution)/shard_map/erd,edf->erf/dot_general | solution.py:32
  315.6 0.0 copy-done
  315.6 36.5 %convolution_convert_fusion = bf16[4096,2048]{1,0:T(8,128)(2,1)} fusion(f32[4096,768]{1,0:T(8,128)} %fusion.3, bf16[4096,2048]{1,0:T(8,128)(2,1)} %bitcast.28, bf16[1,768,2048]{2,1,0:T(8,128)(2,1)S(1)} %copy-done, bf16[1,2048,768]{2,1,0:T(8,128)(2,1)} %param.12), kind=kOutput, calls=%fused_computation.5 | convolution fusion | flops 25797066752 | bytes 52428800 | tf_op jit(solution)/shard_map/erf,efd->erd/dot_general | solution.py:35
  352.1 0.0 copy-start.4
  352.1 0.0 copy-start.6
  352.1 0.0 copy-start.5
  352.1 11.5 %all-to-all-start.1 = ((bf16[1,128,32,2048]{3,2,0,1:T(8,128)(2,1)}), bf16[1,128,32,2048]{3,2,0,1:T(8,128)(2,1)}, u32[]{:S(2)}, u32[]{:S(2)}) async-start(bf16[1,128,32,2048]{3,2,0,1:T(8,128)(2,1)} %bitcast.26), calls=%async_computation.1 | async-start | bytes 33554432 | tf_op jit(solution)/shard_map/all_to_all | solution.py:37
  363.6 0.0 copy-done.4
  363.6 0.1 copy.19
  363.7 0.1 reshape.125
  363.8 0.0 copy-done.6
  363.9 0.2 copy.15
  364.0 0.0 copy-done.5
  364.0 0.1 copy.14
  364.2 285.2 %all-to-all-done.1 = bf16[1,128,32,2048]{3,2,0,1:T(8,128)(2,1)} async-done(((bf16[1,128,32,2048]{3,2,0,1:T(8,128)(2,1)}), bf16[1,128,32,2048]{3,2,0,1:T(8,128)(2,1)}, u32[]{:S(2)}, u32[]{:S(2)}) %all-to-all-start.1) | async-done | bytes 16777248 | tf_op jit(solution)/shard_map/all_to_all | solution.py:37
  649.4 0.0 copy-start.1
  649.4 24.4 %gather_fusion.1 = bf16[2048,2048]{1,0:T(8,128)(2,1)} fusion(bf16[4096,2048]{1,0:T(8,128)(2,1)} %bitcast.9, s32[2048]{0:T(1024)S(1)} %broadcast_clamp_fusion), kind=kCustom, calls=%fused_computation.1 | custom fusion | bytes 16785408 | tf_op jit(solution)/shard_map/jit(_take)/gather | solution.py:39
  673.8 10.3 %multiply_reduce_fusion = bf16[256,2048]{1,0:T(8,128)(2,1)} fusion(bf16[2048,2048]{1,0:T(8,128)(2,1)} %gather_fusion.1, f32[256,8]{1,0:T(8,128)S(1)} %copy.14, pred[256,8]{1,0:T(8,128)(4,1)S(1)} %copy.15), kind=kLoop, calls=%fused_computation.3 | loop fusion | flops 16252928 | bytes 9447424 | tf_op jit(solution)/shard_map/reduce_sum | solution.py:40
  684.2 0.0 copy-done.1
  (6 shorter events, 0.0 us)
Async XLA Ops:
  0.0 315.6 %copy-start = (bf16[1,768,2048]{2,1,0:T(8,128)(2,1)S(1)}, bf16[1,768,2048]{2,1,0:T(8,128)(2,1)}, u32[]{:S(2)}) copy-start(bf16[1,768,2048]{2,1,0:T(8,128)(2,1)} %param.13) | copy-start | bytes 9437188
  1.5 41.3 %copy-start.3 = (s32[256,8]{0,1:T(8,128)}, s32[256,8]{0,1:T(8,128)S(1)}, u32[]{:S(2)}) copy-start(s32[256,8]{0,1:T(8,128)S(1)} %get-tuple-element.6) | copy-start | bytes 24580
  51.0 248.3 %copy-start.7 = (bf16[1,2048,768]{2,1,0:T(8,128)(2,1)S(1)}, bf16[1,2048,768]{2,1,0:T(8,128)(2,1)}, u32[]{:S(2)}) copy-start(bf16[1,2048,768]{2,1,0:T(8,128)(2,1)} %param.11) | copy-start | bytes 9437188
  293.6 5.7 copy-start.2
  352.1 11.5 %copy-start.4 = (s32[256,8]{0,1:T(8,128)S(1)}, s32[256,8]{0,1:T(8,128)}, u32[]{:S(2)}) copy-start(s32[256,8]{0,1:T(8,128)} %copy-done.3) | copy-start | bytes 24580
  352.1 11.7 %copy-start.6 = (pred[256,8]{0,1:T(8,128)(4,1)S(1)}, pred[256,8]{0,1:T(8,128)(4,1)}, u32[]{:S(2)}) copy-start(pred[256,8]{0,1:T(8,128)(4,1)} %get-tuple-element.5) | copy-start | bytes 6148
  352.1 11.9 %copy-start.5 = (f32[256,8]{0,1:T(8,128)S(1)}, f32[256,8]{0,1:T(8,128)}, u32[]{:S(2)}) copy-start(f32[256,8]{0,1:T(8,128)} %param.9) | copy-start | bytes 24580
  352.1 297.3 %all-to-all-start.1 = ((bf16[1,128,32,2048]{3,2,0,1:T(8,128)(2,1)}), bf16[1,128,32,2048]{3,2,0,1:T(8,128)(2,1)}, u32[]{:S(2)}, u32[]{:S(2)}) async-start(bf16[1,128,32,2048]{3,2,0,1:T(8,128)(2,1)} %bitcast.26), calls=%async_computation.1 | async-start | bytes 33554432 | tf_op jit(solution)/shard_map/all_to_all | solution.py:37
  649.4 34.8 %copy-start.1 = (bf16[1,768,2048]{2,1,0:T(8,128)(2,1)S(1)}, bf16[1,768,2048]{2,1,0:T(8,128)(2,1)}, u32[]{:S(2)}) copy-start(bf16[1,768,2048]{2,1,0:T(8,128)(2,1)} %param.13) | copy-start | bytes 9437188
where the time goes:
time: 684 us
  waiting for transfers between devices  285 us (42%)
  blocking collectives  243 us (36%)
  local copies, waits for them, and re-layouts  71.9 us (11%)
  matrix products  52.7 us (8%)
  other arithmetic  20.1 us (3%)
  starting transfers between devices  11.5 us (2%)
    all_to_all x1, waiting for transfers between devices, local_layer(): returned = lax.all_to_all(expert_out, group_axes, 1, 0, tiled=True)  285 us
    all_to_all x1, blocking collectives, local_layer(): recv_buf = lax.all_to_all(send_buf, group_axes, 0, 2, tiled=True)  243 us
    dot_general x1, matrix products, local_layer(): jnp.einsum('erf,efd->erd', hidden, w_down, preferred_element_type=jnp.flo...  36.5 us
    gather x1, local copies, waits for them, and re-layouts, local_layer(): send_buf = jnp.take(tokens, src_table, axis=0, mode='fill', fill_value=0)  32.7 us
    gather x1, local copies, waits for them, and re-layouts, local_layer(): picked = jnp.take(returned, flat_pos, axis=0, mode='fill', fill_value=0)  24.4 us
    dot_general x1, matrix products, local_layer(): jnp.einsum('erd,edf->erf', recv_buf, w_gate, preferred_element_type=jnp.f...  16.2 us
  transfers between devices with their start and end apart: 1, of which 1 were waited for; matrix products, arithmetic and copies ran while one was open for 0% of the time, Pallas kernels for 0%

commit v1 on v0

v1 whole, which is shorter than its diff:
```python
import jax
import jax.numpy as jnp
from jax import lax
from jax.experimental import pallas as pl
from jax.experimental.pallas import tpu as pltpu
from jax.sharding import PartitionSpec as P

MESH = pl.DeviceIdType.MESH
CAP_FACTOR = 2
RING = 4
DELTAS = (1, 3, 2)
COLS = ((0, 768), (768, 640), (1408, 640))
STRIDES = ((16, 4, 1), (4, 1, 16))


def capacity(rows, top_k, experts):
    return ((CAP_FACTOR * rows * top_k + 8 * experts - 1) // (8 * experts)) * 8


def place():
    core, e = lax.axis_index("node"), lax.axis_index("expert")
    z, y, x = e // 16, (e // 4) % 4, e % 4
    return core, e, ((z, y, x), (y, x, z))


def own_view(core, views):
    v = tuple(a + core * (b - a) for a, b in zip(*views))
    s = tuple(a + core * (b - a) for a, b in zip(*STRIDES))
    return v, s


def step(e, pos, stride, delta):
    return e + (lax.rem(pos + delta, RING) - pos) * stride


def cols(k):
    return pl.ds(*COLS[k])


def dims(k):
    return k % 3, (k + 1) % 3, (k + 2) % 3


def plane_at(k, d0, d1):
    return (d1, d0) if k == 2 else (d0, d1)


def cube_at(k, p):
    full = [slice(None)] * 3
    full[dims(k)[2]] = p
    return tuple(full)


def remote(src, dst, send, recv, core, e):
    return pltpu.make_async_remote_copy(src_ref=src, dst_ref=dst, send_sem=send, recv_sem=recv, device_id=(0, core, e), device_id_type=MESH)


def greet(targets):
    barrier = pltpu.get_barrier_semaphore()
    for core, e in targets:
        pl.semaphore_signal(barrier, inc=1, device_id=(0, core, e), device_id_type=MESH)
    pl.semaphore_wait(barrier, len(targets))


def ring_peers(core_list, e, views):
    out = []
    for core in core_list:
        for v, s in zip(views[0], STRIDES[0]):
            for delta in DELTAS:
                out.append((core, step(e, v, s, delta)))
    return out


def spread_kernel(tok, meta, t2, mt, loc, s1s, s1r, m1s, m1r, s2s, s2r, m2s, m2r, s3s, s3r):
    core, e, views = place()
    v, st = own_view(core, views)
    greet(ring_peers((core,), e, views))
    half = tok.shape[0] // 2
    sends, locals_ = [], []

    def go(copy):
        copy.start()
        sends.append(copy)

    for k in range(3):
        i0, i1, _ = dims(k)
        here = plane_at(k, v[i0], v[i1])
        for delta in DELTAS:
            peer = step(e, v[i0], st[i0], delta)
            go(remote(tok.at[:, cols(k)], t2.at[(*here, slice(None), cols(k))], s1s.at[k, delta - 1], s1r.at[k, delta - 1], core, peer))
            go(remote(meta, mt.at[(k, *here)], m1s.at[k, delta - 1], m1r.at[k, delta - 1], core, peer))
    for k in range(3):
        i0, i1, _ = dims(k)
        here = plane_at(k, v[i0], v[i1])
        own = pltpu.make_async_copy(tok.at[:, cols(k)], t2.at[(*here, slice(None), cols(k))], loc.at[0, k])
        own.start()
        locals_.append(own)
        own = pltpu.make_async_copy(meta, mt.at[(k, *here)], loc.at[1, k])
        own.start()
        locals_.append(own)

    def second(k, j):
        i0, i1, _ = dims(k)
        at = plane_at(k, lax.rem(v[i0] + j, RING), v[i1])
        block = t2.at[(*at, slice(None), cols(k))]
        for way, delta in enumerate((1, 3)):
            src = tok.at[:, cols(k)] if j == 0 else block
            go(remote(src, block, s2s.at[k, j, way], s2r.at[k, j, way], core, step(e, v[i1], st[i1], delta)))
        for delta in DELTAS:
            src = meta if j == 0 else mt.at[(k, *at)]
            go(remote(src, mt.at[(k, *at)], m2s.at[k, j, delta - 1], m2r.at[k, j, delta - 1], core, step(e, v[i1], st[i1], delta)))

    for k in range(3):
        second(k, 0)
    for j in DELTAS:
        for k in range(3):
            i0, i1, _ = dims(k)
            at = plane_at(k, lax.rem(v[i0] + j, RING), v[i1])
            block = t2.at[(*at, slice(None), cols(k))]
            remote(block, block, s1s.at[k, 3 - j], s1r.at[k, 3 - j], core, e).wait_recv()
            remote(mt.at[(k, *at)], mt.at[(k, *at)], m1s.at[k, 3 - j], m1r.at[k, 3 - j], core, e).wait_recv()
            second(k, j)
    for j in (0, *DELTAS):
        for k in range(3):
            i0, i1, _ = dims(k)
            for way, delta in enumerate((1, 3)):
                at = plane_at(k, lax.rem(v[i0] + j, RING), lax.rem(v[i1] + 4 - delta, RING))
                block = t2.at[(*at, slice(None), cols(k))]
                remote(block, block, s2s.at[k, j, way], s2r.at[k, j, way], core, e).wait_recv()
                part = t2.at[(*at, pl.ds(half * way, half), cols(k))]
                go(remote(part, part, s3s.at[k, j, way], s3r.at[k, j, way], core, step(e, v[i1], st[i1], delta)))
    for j in (0, *DELTAS):
        for k in range(3):
            i0, i1, _ = dims(k)
            for delta in DELTAS:
                at = plane_at(k, lax.rem(v[i0] + j, RING), lax.rem(v[i1] + 4 - delta, RING))
                remote(mt.at[(k, *at)], mt.at[(k, *at)], m2s.at[k, j, delta - 1], m2r.at[k, j, delta - 1], core, e).wait_recv()
            at = plane_at(k, lax.rem(v[i0] + j, RING), lax.rem(v[i1] + 2, RING))
            for way in range(2):
                part = t2.at[(*at, pl.ds(half * way, half), cols(k))]
                remote(part, part, s3s.at[k, j, way], s3r.at[k, j, way], core, e).wait_recv()
    for copy in sends:
        copy.wait_send()
    for copy in locals_:
        copy.wait()


def pick_kernel(slots, t2, mt, out):
    core, e, views = place()
    v, st = own_view(core, views)
    rows = RING * 2 * slots
    r = lax.broadcasted_iota(jnp.int32, (rows, 1), 0)
    p2, half, s = r // (2 * slots), (r // slots) % 2, r % slots
    for k in range(3):
        i0, i1, i2 = dims(k)
        key = ((half * 64 + v[i0] * st[i0] + v[i1] * st[i1] + p2 * st[i2]) * slots + s).astype(jnp.float32)
        hot = jnp.zeros((rows, t2.shape[2]), jnp.float32)
        for j in range(8):
            hot = jnp.where(key == mt[k, 0, 0, j:j + 1, :], 1.0, hot)
        got = jnp.dot(hot.astype(jnp.bfloat16), t2[0, 0, :, cols(k)], preferred_element_type=jnp.float32)
        out[:, :, 0, 0, :, cols(k)] = got.astype(jnp.bfloat16).reshape(RING, 2, slots, COLS[k][1])


def out_kernel(s_ref, r_ref, bounce, loc, ss, rs):
    core, e, views = place()
    v, st = own_view(core, views)
    greet(ring_peers((0, 1), e, views) + [(1 - core, e)])
    sends = []
    for delta in (1, 3, 2):
        for k in range(3):
            i2 = dims(k)[2]
            p = lax.rem(v[i2] + delta, RING)
            for to in range(2):
                copy = remote(s_ref.at[p, to, :, :, :, cols(k)], r_ref.at[(core, *cube_at(k, v[i2]), slice(None), cols(k))], ss.at[k, delta, to], rs.at[k, delta, core], to, step(e, v[i2], st[i2], delta))
                copy.start()
                sends.append(copy)
    ins, outs = [], []
    for k in range(3):
        i2 = dims(k)[2]
        target = r_ref.at[(core, *cube_at(k, v[i2]), slice(None), cols(k))]
        copy = remote(s_ref.at[v[i2], 1 - core, :, :, :, cols(k)], target, ss.at[k, 0, 0], rs.at[k, 0, 0], 1 - core, e)
        copy.start()
        sends.append(copy)
        room = bounce.at[:, :, :, cols(k)]
        into = pltpu.make_async_copy(s_ref.at[v[i2], core, :, :, :, cols(k)], room, loc.at[0, k])
        into.start()
        ins.append(into)
        outs.append(pltpu.make_async_copy(room, target, loc.at[1, k]))
    for into, out in zip(ins, outs):
        into.wait()
        out.start()
    for out in outs:
        out.wait()
    other = own_view(1 - core, views)[0]
    for k in range(3):
        i2 = dims(k)[2]
        target = r_ref.at[(1 - core, *cube_at(k, other[i2]), slice(None), cols(k))]
        remote(target, target, ss.at[k, 0, 0], rs.at[k, 0, 0], core, e).wait_recv()
        for delta in (1, 3, 2):
            for o in range(2):
                target = r_ref.at[(o, *cube_at(k, lax.rem(views[o][i2] + 4 - delta, RING)), slice(None), cols(k))]
                remote(target, target, ss.at[k, delta, 0], rs.at[k, delta, o], core, e).wait_recv()
    for copy in sends:
        copy.wait_send()


def back_kernel(y_ref, z4, z5, bounce, bounce2, loc, s4, r4, s5, r5):
    core, e, views = place()
    v, st = own_view(core, views)
    greet(ring_peers((0, 1), e, views) + [(1 - core, e)])
    sends = []
    for delta in (1, 3, 2):
        for k in range(3):
            i2 = dims(k)[2]
            for o in range(2):
                here = views[o][i2]
                copy = remote(y_ref.at[(o, *cube_at(k, lax.rem(here + delta, RING)), slice(None), cols(k))], z4.at[here, core, :, :, :, cols(k)], s4.at[k, delta, o], r4.at[k, delta, core], o, step(e, here, STRIDES[o][i2], delta))
                copy.start()
                sends.append(copy)
    other = own_view(1 - core, views)[0]
    ins, outs = [], []
    for k in range(3):
        i2 = dims(k)[2]
        copy = remote(y_ref.at[(1 - core, *cube_at(k, other[i2]), slice(None), cols(k))], z4.at[other[i2], core, :, :, :, cols(k)], s4.at[k, 0, 0], r4.at[k, 0, 0], 1 - core, e)
        copy.start()
        sends.append(copy)
        room = bounce.at[:, :, :, cols(k)]
        into = pltpu.make_async_copy(y_ref.at[(core, *cube_at(k, v[i2]), slice(None), cols(k))], room, loc.at[0, k])
        into.start()
        ins.append(into)
        outs.append(pltpu.make_async_copy(room, z4.at[v[i2], core, :, :, :, cols(k)], loc.at[1, k]))
    for into, out in zip(ins, outs):
        into.wait()
        out.start()
    for out in outs:
        out.wait()

    def line(k, q):
        at = (slice(None), slice(None), q, slice(None)) if k == 2 else (slice(None), slice(None), slice(None), q)
        return z4.at[(*at, slice(None), cols(k))]

    ins, outs = [], []
    for k in range(3):
        i1, i2 = dims(k)[1:]
        target = z4.at[v[i2], 1 - core, :, :, :, cols(k)]
        remote(target, target, s4.at[k, 0, 0], r4.at[k, 0, 0], core, e).wait_recv()
        for delta in (1, 3, 2):
            for o in range(2):
                target = z4.at[lax.rem(v[i2] + 4 - delta, RING), o, :, :, :, cols(k)]
                remote(target, target, s4.at[k, delta, 0], r4.at[k, delta, o], core, e).wait_recv()
        for delta in (1, 3, 2):
            copy = remote(line(k, lax.rem(v[i1] + delta, RING)), z5.at[v[i1], :, :, :, :, cols(k)], s5.at[k, delta - 1], r5.at[k, delta - 1], core, step(e, v[i1], st[i1], delta))
            copy.start()
            sends.append(copy)
        room = bounce2.at[:, :, :, :, cols(k)]
        into = pltpu.make_async_copy(line(k, v[i1]), room, loc.at[2, k])
        into.start()
        ins.append(into)
        outs.append(pltpu.make_async_copy(room, z5.at[v[i1], :, :, :, :, cols(k)], loc.at[3, k]))
    for into, out in zip(ins, outs):
        into.wait()
        out.start()
    for out in outs:
        out.wait()
    for k in range(3):
        i1 = dims(k)[1]
        for delta in (1, 3, 2):
            target = z5.at[lax.rem(v[i1] + 4 - delta, RING), :, :, :, :, cols(k)]
            remote(target, target, s5.at[k, delta - 1], r5.at[k, delta - 1], core, e).wait_recv()
    for copy in sends:
        copy.wait_send()


def weigh_kernel(slots, z5, mt, out):
    core, e, views = place()
    v, st = own_view(core, views)
    d0 = pl.program_id(0)
    n = RING * RING * 2 * slots
    r = lax.broadcasted_iota(jnp.int32, (1, n), 1)
    d1, p2, half, s = r // (RING * 2 * slots), (r // (2 * slots)) % RING, (r // slots) % 2, r % slots
    for k in range(3):
        i0, i1, i2 = dims(k)
        a, b = plane_at(k, d0, v[i1])
        m = jnp.transpose(mt[k, a, b])
        key = ((half * 64 + v[i0] * st[i0] + d1 * st[i1] + p2 * st[i2]) * slots + s).astype(jnp.float32)
        w = jnp.zeros((m.shape[0], n), jnp.float32)
        for j in range(8):
            w = jnp.where(m[:, j:j + 1] == key, m[:, 8 + j:9 + j], w)
        hi = w.astype(jnp.bfloat16)
        rest = w - hi.astype(jnp.float32)
        mid = rest.astype(jnp.bfloat16)
        low = (rest - mid.astype(jnp.float32)).astype(jnp.bfloat16)
        y = z5[:, :, :, 0, :, cols(k)].reshape(n, COLS[k][1])
        total = jnp.dot(low, y, preferred_element_type=jnp.float32)
        total += jnp.dot(mid, y, preferred_element_type=jnp.float32)
        total += jnp.dot(hi, y, preferred_element_type=jnp.float32)
        out[0, :, cols(k)] = total


def sum_kernel(p_ref, out, q, loc, ss, rs):
    core, e, views = place()
    v, st = own_view(core, views)
    greet(ring_peers((core,), e, views))
    sends, locals_ = [], []
    for delta in (1, 3, 2):
        for k in range(3):
            i0 = dims(k)[0]
            copy = remote(p_ref.at[lax.rem(v[i0] + delta, RING), :, cols(k)], q.at[delta, :, cols(k)], ss.at[k, delta - 1], rs.at[k, delta - 1], core, step(e, v[i0], st[i0], delta))
            copy.start()
            sends.append(copy)
    for k in range(3):
        copy = pltpu.make_async_copy(p_ref.at[v[dims(k)[0]], :, cols(k)], q.at[0, :, cols(k)], loc.at[k])
        copy.start()
        locals_.append(copy)
    for copy in locals_:
        copy.wait()
    for k in range(3):
        for delta in (1, 3, 2):
            target = q.at[delta, :, cols(k)]
            remote(target, target, ss.at[k, delta - 1], rs.at[k, delta - 1], core, e).wait_recv()

    @pl.loop(0, out.shape[0] // 16)
    def _(i):
        at = pl.ds(pl.multiple_of(i * 16, 16), 16)
        out[at, :] = ((q[0, at, :] + q[1, at, :]) + (q[2, at, :] + q[3, at, :])).astype(jnp.bfloat16)

    for copy in sends:
        copy.wait_send()


def comm_call(body, name, cid, ins, outs, scratch):
    return pl.pallas_call(
        body,
        name=name,
        out_shape=outs,
        in_specs=ins,
        out_specs=[pl.BlockSpec(memory_space=pltpu.HBM)] * len(outs) if isinstance(outs, list) else pl.BlockSpec(memory_space=pltpu.VMEM),
        scratch_shapes=scratch,
        compiler_params=pltpu.CompilerParams(collective_id=cid, has_side_effects=True),
    )


def solution(mesh):
    group_axes = ("node", "expert")
    group_size = mesh.shape["node"] * mesh.shape["expert"]
    tok_spec = P(("data", "node", "expert"), None)
    weight_spec = P(("node", "expert"), None, None)
    hbm = pl.BlockSpec(memory_space=pltpu.HBM)
    vmem = pl.BlockSpec(memory_space=pltpu.VMEM)
    dma = pltpu.SemaphoreType.DMA

    def local_layer(tokens, expert_ids, gate_weights, slot_ids, w_gate, w_up, w_down):
        rows, width = tokens.shape
        top_k = expert_ids.shape[1]
        slots = capacity(rows, top_k, group_size)
        bf = jnp.bfloat16
        pos = jnp.where(slot_ids >= 0, expert_ids * slots + slot_ids, -1).astype(jnp.float32)
        meta = jnp.concatenate([pos.T, gate_weights.T], axis=0)
        t2, mt = comm_call(
            spread_kernel, "spread", 1, [vmem, vmem],
            [jax.ShapeDtypeStruct((4, 4, rows, width), bf), jax.ShapeDtypeStruct((3, 4, 4, 16, rows), jnp.float32)],
            [dma((2, 3))] + [dma((3, 3))] * 4 + [dma((3, 4, 2))] * 2 + [dma((3, 4, 3))] * 2 + [dma((3, 4, 2))] * 2,
        )(tokens, meta)
        s = pl.pallas_call(
            lambda *refs: pick_kernel(slots, *refs),
            name="pick",
            grid=(4, 4),
            in_specs=[pl.BlockSpec((1, 1, rows, width), lambda a, b: (a, b, 0, 0)), pl.BlockSpec((3, 1, 1, 16, rows), lambda a, b: (0, a, b, 0, 0))],
            out_specs=pl.BlockSpec((4, 2, 1, 1, slots, width), lambda a, b: (0, 0, a, b, 0, 0)),
            out_shape=jax.ShapeDtypeStruct((4, 2, 4, 4, slots, width), bf),
        )(t2, mt)
        (r,) = comm_call(
            out_kernel, "send_out", 2, [hbm],
            [jax.ShapeDtypeStruct((2, 4, 4, 4, slots, width), bf)],
            [pltpu.VMEM((4, 4, slots, width), bf), dma((2, 3)), dma((3, 4, 2)), dma((3, 4, 2))],
        )(s)
        r = r.reshape(group_size * slots, width)
        proj_gate = jnp.dot(r, w_gate[0], preferred_element_type=jnp.float32)
        proj_up = jnp.dot(r, w_up[0], preferred_element_type=jnp.float32)
        hidden = (jax.nn.silu(proj_gate) * proj_up).astype(bf)
        y = jnp.dot(hidden, w_down[0], preferred_element_type=jnp.float32).astype(bf)
        y = y.reshape(2, 4, 4, 4, slots, width)
        z4, z5 = comm_call(
            back_kernel, "send_back", 3, [hbm],
            [jax.ShapeDtypeStruct((4, 2, 4, 4, slots, width), bf), jax.ShapeDtypeStruct((4, 4, 2, 4, slots, width), bf)],
            [pltpu.VMEM((4, 4, slots, width), bf), pltpu.VMEM((4, 2, 4, slots, width), bf), dma((4, 3)), dma((3, 4, 2)), dma((3, 4, 2)), dma((3, 3)), dma((3, 3))],
        )(y)
        part = pl.pallas_call(
            lambda *refs: weigh_kernel(slots, *refs),
            name="weigh",
            grid=(4,),
            in_specs=[pl.BlockSpec((4, 4, 2, 1, slots, width), lambda d: (0, 0, 0, d, 0, 0)), pl.BlockSpec((3, 4, 4, 16, rows), lambda d: (0, 0, 0, 0, 0))],
            out_specs=pl.BlockSpec((1, rows, width), lambda d: (d, 0, 0)),
            out_shape=jax.ShapeDtypeStruct((4, rows, width), jnp.float32),
        )(z5, mt)
        return comm_call(
            sum_kernel, "sum_up", 4, [hbm], jax.ShapeDtypeStruct((rows, width), bf),
            [pltpu.VMEM((4, rows, width), jnp.float32), dma((3,)), dma((3, 3)), dma((3, 3))],
        )(part)

    return jax.shard_map(local_layer, mesh=mesh, in_specs=(tok_spec, tok_spec, tok_spec, tok_spec, weight_spec, weight_spec, weight_spec), out_specs=tok_spec, check_vma=False)
```

time: 684 us -> 419 us (0.61)
  the two profiles are of different devices: /device:TPU:39 before, /device:TPU:1 now
where the time goes in v1:
time: 419 us
  Pallas kernels  358 us (85%)
  matrix products  55.7 us (13%)
    pallas_call x1, Pallas kernels, local_layer(): comm_call(back_kernel, 'send_back', 3, [hbm], [jax.ShapeDtypeStruct((4, 2...  129 us
    pallas_call x1, Pallas kernels, local_layer(): comm_call(spread_kernel, 'spread', 1, [vmem, vmem], [jax.ShapeDtypeStruct...  75.6 us
    pallas_call x1, Pallas kernels, local_layer(): comm_call(out_kernel, 'send_out', 2, [hbm], [jax.ShapeDtypeStruct((2, 4,...  69.3 us
    pallas_call x1, Pallas kernels, local_layer(): comm_call(sum_kernel, 'sum_up', 4, [hbm], jax.ShapeDtypeStruct((rows, wid...  36.5 us
    dot_general x1, matrix products, local_layer(): jnp.dot(hidden, w_down[0], preferred_element_type=jnp.float32).astype(bf)  36.5 us
    pallas_call x1, Pallas kernels, local_layer(): pl.pallas_call(lambda *refs: weigh_kernel(slots, *refs), name='weigh', gr...  26.6 us
    pallas_call x1, Pallas kernels, local_layer(): pl.pallas_call(lambda *refs: pick_kernel(slots, *refs), name='pick', grid...  21.7 us
    dot_general x1, matrix products, local_layer(): proj_gate = jnp.dot(r, w_gate[0], preferred_element_type=jnp.float32)  19.3 us

profile of v1, /device:TPU:1, one launch (start us, length us, event | category | flops | bytes accessed | tf_op | source)
XLA Modules:
  0.0 418.7 jit_solution(2335614882983261503)
XLA Ops:
  0.0 0.0 copy-start
  0.0 0.9 convert_bitcast_fusion
  0.9 1.4 pad_maximum_fusion.meta
  2.3 75.6 %spread.1 = (bf16[4,4,256,2048]{3,2,1,0:T(8,128)(2,1)}, f32[3,4,4,16,256]{4,3,2,1,0:T(8,128)}) custom-call(bf16[256,2048]{1,0:T(8,128)(2,1)} %tok.1, f32[16,256]{1,0:T(8,128)} %pad_maximum_fusion.meta), custom_call_target="tpu_custom_call" | custom-call | tf_op jit(solution)/shard_map/spread/pallas_call | solution.py:359
  77.9 21.7 %pick.1.s_ref = bf16[4,2,4,4,32,2048]{5,4,3,2,1,0:T(8,128)(2,1)} custom-call(bf16[4,4,256,2048]{3,2,1,0:T(8,128)(2,1)} %get-tuple-element.8.refs_0_, f32[3,4,4,16,256]{4,3,2,1,0:T(8,128)} %get-tuple-element.9.refs_1_), custom_call_target="tpu_custom_call" | custom-call | tf_op jit(solution)/shard_map/pick/pallas_call | solution.py:364
  99.6 69.3 %send_out.1 = bf16[2,4,4,4,32,2048]{5,4,3,2,1,0:T(8,128)(2,1)} custom-call(bf16[4,2,4,4,32,2048]{5,4,3,2,1,0:T(8,128)(2,1)} %pick.1.s_ref), custom_call_target="tpu_custom_call" | custom-call | tf_op jit(solution)/shard_map/send_out/pallas_call | solution.py:372
  168.9 19.3 %fusion.3 = f32[4096,768]{1,0:T(8,128)} fusion(bf16[4096,2048]{1,0:T(8,128)(2,1)} %bitcast.18, bf16[1,2048,768]{2,1,0:T(8,128)(2,1)} %param.11), kind=kOutput, calls=%fused_computation.4 | convolution fusion | flops 12884901888 | bytes 32505856 | tf_op jit(solution)/shard_map/dot_general | solution.py:378
  188.2 0.0 copy-done
  188.2 36.5 %convolution_convert_fusion = bf16[4096,2048]{1,0:T(8,128)(2,1)} fusion(f32[4096,768]{1,0:T(8,128)} %fusion.3, bf16[4096,2048]{1,0:T(8,128)(2,1)} %bitcast.19, bf16[1,768,2048]{2,1,0:T(8,128)(2,1)S(1)} %copy-done, bf16[1,2048,768]{2,1,0:T(8,128)(2,1)} %param.12), kind=kOutput, calls=%fused_computation | convolution fusion | flops 25797066752 | bytes 52428800 | tf_op jit(solution)/shard_map/dot_general | solution.py:381
  224.7 128.6 %send_back.1 = (bf16[4,2,4,4,32,2048]{5,4,3,2,1,0:T(8,128)(2,1)}, bf16[4,4,2,4,32,2048]{5,4,3,2,1,0:T(8,128)(2,1)}) custom-call(bf16[2,4,4,4,32,2048]{5,4,3,2,1,0:T(8,128)(2,1)} %bitcast.17), custom_call_target="tpu_custom_call" | custom-call | tf_op jit(solution)/shard_map/send_back/pallas_call | solution.py:383
  353.3 0.0 copy-start.1
  353.3 26.6 %weigh.1.p_ref = f32[4,256,2048]{2,1,0:T(8,128)} custom-call(bf16[4,4,2,4,32,2048]{5,4,3,2,1,0:T(8,128)(2,1)} %get-tuple-element.10.refs_0_, f32[3,4,4,16,256]{4,3,2,1,0:T(8,128)} %get-tuple-element.9.refs_1_), custom_call_target="tpu_custom_call" | custom-call | tf_op jit(solution)/shard_map/weigh/pallas_call | solution.py:388
  379.9 36.5 %sum_up.1 = bf16[256,2048]{1,0:T(8,128)(2,1)} custom-call(f32[4,256,2048]{2,1,0:T(8,128)} %weigh.1.p_ref), custom_call_target="tpu_custom_call" | custom-call | tf_op jit(solution)/shard_map/sum_up/pallas_call | solution.py:396
  416.4 2.3 copy.9
  418.7 0.0 copy-done.1
Async XLA Ops:
  0.0 188.2 %copy-start = (bf16[1,768,2048]{2,1,0:T(8,128)(2,1)S(1)}, bf16[1,768,2048]{2,1,0:T(8,128)(2,1)}, u32[]{:S(2)}) copy-start(bf16[1,768,2048]{2,1,0:T(8,128)(2,1)} %param.13) | copy-start | bytes 9437188
  353.3 65.5 %copy-start.1 = (bf16[1,768,2048]{2,1,0:T(8,128)(2,1)S(1)}, bf16[1,768,2048]{2,1,0:T(8,128)(2,1)}, u32[]{:S(2)}) copy-start(bf16[1,768,2048]{2,1,0:T(8,128)(2,1)} %param.13) | copy-start | bytes 9437188

commit v2 on v1

v2 whole, which is shorter than its diff:
```python
import jax
import jax.numpy as jnp
from jax import lax
from jax.experimental import pallas as pl
from jax.experimental.pallas import tpu as pltpu
from jax.sharding import PartitionSpec as P

MESH = pl.DeviceIdType.MESH
CAP_FACTOR = 2
RING = 4
DELTAS = (1, 3, 2)
COLS = ((0, 768), (768, 640), (1408, 640))
STRIDES = ((16, 4, 1), (4, 1, 16))


def capacity(rows, top_k, experts):
    return ((CAP_FACTOR * rows * top_k + 8 * experts - 1) // (8 * experts)) * 8


def place():
    core, e = lax.axis_index("node"), lax.axis_index("expert")
    z, y, x = e // 16, (e // 4) % 4, e % 4
    return core, e, ((z, y, x), (y, x, z))


def own_view(core, views):
    v = tuple(a + core * (b - a) for a, b in zip(*views))
    s = tuple(a + core * (b - a) for a, b in zip(*STRIDES))
    return v, s


def step(e, pos, stride, delta):
    return e + (lax.rem(pos + delta, RING) - pos) * stride


def cols(k):
    return pl.ds(*COLS[k])


def dims(k):
    return k % 3, (k + 1) % 3, (k + 2) % 3


def plane_at(k, d0, d1):
    return (d1, d0) if k == 2 else (d0, d1)


def cube_at(k, p):
    full = [slice(None)] * 3
    full[dims(k)[2]] = p
    return tuple(full)


def remote(src, dst, send, recv, core, e):
    return pltpu.make_async_remote_copy(src_ref=src, dst_ref=dst, send_sem=send, recv_sem=recv, device_id=(0, core, e), device_id_type=MESH)


def greet(targets):
    barrier = pltpu.get_barrier_semaphore()
    for core, e in targets:
        pl.semaphore_signal(barrier, inc=1, device_id=(0, core, e), device_id_type=MESH)
    pl.semaphore_wait(barrier, len(targets))


def ring_peers(core_list, e, views):
    out = []
    for core in core_list:
        for v, s in zip(views[0], STRIDES[0]):
            for delta in DELTAS:
                out.append((core, step(e, v, s, delta)))
    return out


def spread_kernel(tok, meta, t2, mt, loc, s1s, s1r, m1s, m1r, s2s, s2r, m2s, m2r, s3s, s3r):
    core, e, views = place()
    v, st = own_view(core, views)
    greet(ring_peers((core,), e, views))
    half = tok.shape[0] // 2
    sends, locals_ = [], []

    def go(copy):
        copy.start()
        sends.append(copy)

    for k in range(3):
        i0, i1, _ = dims(k)
        here = plane_at(k, v[i0], v[i1])
        for delta in DELTAS:
            peer = step(e, v[i0], st[i0], delta)
            go(remote(tok.at[:, cols(k)], t2.at[(*here, slice(None), cols(k))], s1s.at[k, delta - 1], s1r.at[k, delta - 1], core, peer))
            go(remote(meta, mt.at[(k, *here)], m1s.at[k, delta - 1], m1r.at[k, delta - 1], core, peer))
    for k in range(3):
        i0, i1, _ = dims(k)
        here = plane_at(k, v[i0], v[i1])
        own = pltpu.make_async_copy(tok.at[:, cols(k)], t2.at[(*here, slice(None), cols(k))], loc.at[0, k])
        own.start()
        locals_.append(own)
        own = pltpu.make_async_copy(meta, mt.at[(k, *here)], loc.at[1, k])
        own.start()
        locals_.append(own)

    def second(k, j):
        i0, i1, _ = dims(k)
        at = plane_at(k, lax.rem(v[i0] + j, RING), v[i1])
        block = t2.at[(*at, slice(None), cols(k))]
        for way, delta in enumerate((1, 3)):
            src = tok.at[:, cols(k)] if j == 0 else block
            go(remote(src, block, s2s.at[k, j, way], s2r.at[k, j, way], core, step(e, v[i1], st[i1], delta)))
        for delta in DELTAS:
            src = meta if j == 0 else mt.at[(k, *at)]
            go(remote(src, mt.at[(k, *at)], m2s.at[k, j, delta - 1], m2r.at[k, j, delta - 1], core, step(e, v[i1], st[i1], delta)))

    for k in range(3):
        second(k, 0)
    for j in DELTAS:
        for k in range(3):
            i0, i1, _ = dims(k)
            at = plane_at(k, lax.rem(v[i0] + j, RING), v[i1])
            block = t2.at[(*at, slice(None), cols(k))]
            remote(block, block, s1s.at[k, 3 - j], s1r.at[k, 3 - j], core, e).wait_recv()
            remote(mt.at[(k, *at)], mt.at[(k, *at)], m1s.at[k, 3 - j], m1r.at[k, 3 - j], core, e).wait_recv()
            second(k, j)
    for j in (0, *DELTAS):
        for k in range(3):
            i0, i1, _ = dims(k)
            for way, delta in enumerate((1, 3)):
                at = plane_at(k, lax.rem(v[i0] + j, RING), lax.rem(v[i1] + 4 - delta, RING))
                block = t2.at[(*at, slice(None), cols(k))]
                remote(block, block, s2s.at[k, j, way], s2r.at[k, j, way], core, e).wait_recv()
                part = t2.at[(*at, pl.ds(half * way, half), cols(k))]
                go(remote(part, part, s3s.at[k, j, way], s3r.at[k, j, way], core, step(e, v[i1], st[i1], delta)))
    for j in (0, *DELTAS):
        for k in range(3):
            i0, i1, _ = dims(k)
            for delta in DELTAS:
                at = plane_at(k, lax.rem(v[i0] + j, RING), lax.rem(v[i1] + 4 - delta, RING))
                remote(mt.at[(k, *at)], mt.at[(k, *at)], m2s.at[k, j, delta - 1], m2r.at[k, j, delta - 1], core, e).wait_recv()
            at = plane_at(k, lax.rem(v[i0] + j, RING), lax.rem(v[i1] + 2, RING))
            for way in range(2):
                part = t2.at[(*at, pl.ds(half * way, half), cols(k))]
                remote(part, part, s3s.at[k, j, way], s3r.at[k, j, way], core, e).wait_recv()
    for copy in sends:
        copy.wait_send()
    for copy in locals_:
        copy.wait()


def pick_kernel(slots, t2, mt, out):
    core, e, views = place()
    v, st = own_view(core, views)
    rows = RING * 2 * slots
    r = lax.broadcasted_iota(jnp.int32, (rows, 1), 0)
    p2, half, s = r // (2 * slots), (r // slots) % 2, r % slots
    for k in range(3):
        i0, i1, i2 = dims(k)
        key = ((half * 64 + v[i0] * st[i0] + v[i1] * st[i1] + p2 * st[i2]) * slots + s).astype(jnp.float32)
        hot = jnp.zeros((rows, t2.shape[2]), jnp.float32)
        for j in range(8):
            hot = jnp.where(key == mt[k, 0, 0, j:j + 1, :], 1.0, hot)
        got = jnp.dot(hot.astype(jnp.bfloat16), t2[0, 0, :, cols(k)], preferred_element_type=jnp.float32)
        out[:, :, 0, 0, :, cols(k)] = got.astype(jnp.bfloat16).reshape(RING, 2, slots, COLS[k][1])


def expert_kernel(slots, s_ref, wg_ref, wu_ref, wd_ref, z5, r, z4, wg, wu, wd, wsem, loc, s3, r3, s4, r4, s5, r5):
    core, e, views = place()
    v, st = own_view(core, views)
    other = own_view(1 - core, views)[0]
    part = slots // 2
    loads = [pltpu.make_async_copy(src.at[0], dst, wsem.at[i]) for i, (src, dst) in enumerate(((wg_ref, wg), (wu_ref, wu), (wd_ref, wd)))]
    for load in loads:
        load.start()
    greet(ring_peers((0, 1), e, views) + [(1 - core, e)])
    sends = []

    def go(copy):
        copy.start()
        sends.append(copy)

    def cube(q, o, k, p):
        return r.at[(q, o, *cube_at(k, p), slice(None), cols(k))]

    def inward(q, k):
        i2 = dims(k)[2]
        return pltpu.make_async_copy(s_ref.at[v[i2], core, :, :, pl.ds(part * q, part), cols(k)], cube(q, core, k, v[i2]), loc.at[0, q, k])

    for q in range(2):
        at = pl.ds(part * q, part)
        for delta in DELTAS:
            for k in range(3):
                i2 = dims(k)[2]
                for to in range(2):
                    go(remote(s_ref.at[lax.rem(v[i2] + delta, RING), to, :, :, at, cols(k)], cube(q, core, k, v[i2]), s3.at[q, k, delta, to], r3.at[q, k, delta, core], to, step(e, v[i2], st[i2], delta)))
        for k in range(3):
            i2 = dims(k)[2]
            go(remote(s_ref.at[v[i2], 1 - core, :, :, at, cols(k)], cube(q, core, k, v[i2]), s3.at[q, k, 0, 0], r3.at[q, k, 0, 0], 1 - core, e))
            inward(q, k).start()
    for load in loads:
        load.wait()

    def z4_at(q, k, p, c):
        return z4.at[q, p, c, :, :, :, cols(k)]

    def back(q, o, k, delta):
        i2 = dims(k)[2]
        here = views[o][i2]
        return remote(cube(q, o, k, lax.rem(here + delta, RING)), z4_at(q, k, here, core), s4.at[q, k, delta, o], r4.at[q, k, delta, core], o, step(e, here, STRIDES[o][i2], delta))

    def across(q, k):
        i2 = dims(k)[2]
        return remote(cube(q, 1 - core, k, other[i2]), z4_at(q, k, other[i2], core), s4.at[q, k, 0, 0], r4.at[q, k, 0, 0], 1 - core, e)

    def stay(q, k):
        i2 = dims(k)[2]
        return pltpu.make_async_copy(cube(q, core, k, v[i2]), z4_at(q, k, v[i2], core), loc.at[1, q, k])

    @pl.loop(0, 2)
    def _(q):
        for k in range(3):
            i2 = dims(k)[2]
            inward(q, k).wait()
            target = cube(q, 1 - core, k, other[i2])
            remote(target, target, s3.at[q, k, 0, 0], r3.at[q, k, 0, 0], core, e).wait_recv()
            for delta in DELTAS:
                for o in range(2):
                    target = cube(q, o, k, lax.rem(views[o][i2] + 4 - delta, RING))
                    remote(target, target, s3.at[q, k, delta, 0], r3.at[q, k, delta, o], core, e).wait_recv()
        for o in range(2):
            @pl.loop(0, RING)
            def _(i):
                x = r[q, o, i].reshape(RING * RING * part, r.shape[-1])
                gate = jnp.dot(x, wg[...], preferred_element_type=jnp.float32)
                up = jnp.dot(x, wu[...], preferred_element_type=jnp.float32)
                hidden = (jax.nn.silu(gate) * up).astype(jnp.bfloat16)
                y = jnp.dot(hidden, wd[...], preferred_element_type=jnp.float32).astype(jnp.bfloat16)
                r[q, o, i] = y.reshape(RING, RING, part, r.shape[-1])

            for delta in DELTAS:
                for k in range(3):
                    back(q, o, k, delta).start()
        for k in range(3):
            across(q, k).start()
            stay(q, k).start()

    def line(q, k, p):
        at = (slice(None), slice(None), p, slice(None)) if k == 2 else (slice(None), slice(None), slice(None), p)
        return z4.at[(q, *at, slice(None), cols(k))]

    keep = []
    for q in range(2):
        at = pl.ds(part * q, part)
        for k in range(3):
            i1, i2 = dims(k)[1:]
            stay(q, k).wait()
            target = z4_at(q, k, v[i2], 1 - core)
            remote(target, target, s4.at[q, k, 0, 0], r4.at[q, k, 0, 0], core, e).wait_recv()
            for delta in DELTAS:
                for o in range(2):
                    target = z4_at(q, k, lax.rem(v[i2] + 4 - delta, RING), o)
                    remote(target, target, s4.at[q, k, delta, 0], r4.at[q, k, delta, o], core, e).wait_recv()
            for delta in DELTAS:
                go(remote(line(q, k, lax.rem(v[i1] + delta, RING)), z5.at[v[i1], :, :, :, at, cols(k)], s5.at[q, k, delta - 1], r5.at[q, k, delta - 1], core, step(e, v[i1], st[i1], delta)))
            own = pltpu.make_async_copy(line(q, k, v[i1]), z5.at[v[i1], :, :, :, at, cols(k)], loc.at[2, q, k])
            own.start()
            keep.append(own)
    for own in keep:
        own.wait()
    for q in range(2):
        at = pl.ds(part * q, part)
        for k in range(3):
            i1 = dims(k)[1]
            for delta in DELTAS:
                target = z5.at[lax.rem(v[i1] + 4 - delta, RING), :, :, :, at, cols(k)]
                remote(target, target, s5.at[q, k, delta - 1], r5.at[q, k, delta - 1], core, e).wait_recv()
    for q in range(2):
        for k in range(3):
            across(q, k).wait_send()
            for delta in DELTAS:
                for o in range(2):
                    back(q, o, k, delta).wait_send()
    for copy in sends:
        copy.wait_send()


def sum_kernel(slots, z5, mt, out, zb, part, q, load, own_sem, ss, rs):
    core, e, views = place()
    v, st = own_view(core, views)
    n = RING * RING * 2 * slots
    def fetch(turn, k):
        i0 = dims(k)[0]
        h = turn // 2
        delta = (1 - h) * (2 - turn) + h * (9 - 3 * turn)
        d0 = lax.rem(v[i0] + delta, RING)
        return delta, pltpu.make_async_copy(z5.at[:, :, :, d0, :, cols(k)], zb.at[lax.rem(turn, 2), :, :, :, :, cols(k)], load.at[lax.rem(turn, 2), k])

    def push(delta, k):
        i0 = dims(k)[0]
        return remote(part.at[delta, :, cols(k)], q.at[delta - 1, :, cols(k)], ss.at[k, delta - 1], rs.at[k, delta - 1], core, step(e, v[i0], st[i0], delta))

    for k in range(3):
        fetch(0, k)[1].start()
    greet(ring_peers((core,), e, views))
    r = lax.broadcasted_iota(jnp.int32, (1, n), 1)
    d1, p2, half, s = r // (RING * 2 * slots), (r // (2 * slots)) % RING, (r // slots) % 2, r % slots

    @pl.loop(0, 4)
    def _(turn):
        @pl.when(turn < 3)
        def _():
            for k in range(3):
                fetch(turn + 1, k)[1].start()

        for k in range(3):
            delta, copy = fetch(turn, k)
            copy.wait()
            i0, i1, i2 = dims(k)
            a, b = plane_at(k, lax.rem(v[i0] + delta, RING), v[i1])
            m = jnp.transpose(mt[k, a, b])
            key = ((half * 64 + v[i0] * st[i0] + d1 * st[i1] + p2 * st[i2]) * slots + s).astype(jnp.float32)
            w = jnp.zeros((m.shape[0], n), jnp.float32)
            for j in range(8):
                w = jnp.where(m[:, j:j + 1] == key, m[:, 8 + j:9 + j], w)
            hi = w.astype(jnp.bfloat16)
            rest = w - hi.astype(jnp.float32)
            mid = rest.astype(jnp.bfloat16)
            low = (rest - mid.astype(jnp.float32)).astype(jnp.bfloat16)
            y = zb[lax.rem(turn, 2), :, :, :, :, cols(k)].reshape(n, COLS[k][1])
            total = jnp.dot(low, y, preferred_element_type=jnp.float32)
            total += jnp.dot(mid, y, preferred_element_type=jnp.float32)
            total += jnp.dot(hi, y, preferred_element_type=jnp.float32)
            part[delta, :, cols(k)] = total

            @pl.when(turn < 3)
            def _():
                push(delta, k).start()

    for delta in DELTAS:
        for k in range(3):
            target = q.at[delta - 1, :, cols(k)]
            remote(target, target, ss.at[k, delta - 1], rs.at[k, delta - 1], core, e).wait_recv()

    @pl.loop(0, out.shape[0] // 16)
    def _(i):
        at = pl.ds(pl.multiple_of(i * 16, 16), 16)
        out[at, :] = ((part[0, at, :] + q[0, at, :]) + (q[1, at, :] + q[2, at, :])).astype(jnp.bfloat16)

    for delta in DELTAS:
        for k in range(3):
            push(delta, k).wait_send()


def comm_call(body, name, cid, ins, outs, scratch):
    return pl.pallas_call(
        body,
        name=name,
        out_shape=outs,
        in_specs=ins,
        out_specs=[pl.BlockSpec(memory_space=pltpu.HBM)] * len(outs) if isinstance(outs, list) else pl.BlockSpec(memory_space=pltpu.VMEM),
        scratch_shapes=scratch,
        compiler_params=pltpu.CompilerParams(collective_id=cid, has_side_effects=True),
    )


def solution(mesh):
    group_axes = ("node", "expert")
    group_size = mesh.shape["node"] * mesh.shape["expert"]
    tok_spec = P(("data", "node", "expert"), None)
    weight_spec = P(("node", "expert"), None, None)
    hbm = pl.BlockSpec(memory_space=pltpu.HBM)
    vmem = pl.BlockSpec(memory_space=pltpu.VMEM)
    dma = pltpu.SemaphoreType.DMA

    def local_layer(tokens, expert_ids, gate_weights, slot_ids, w_gate, w_up, w_down):
        rows, width = tokens.shape
        top_k = expert_ids.shape[1]
        slots = capacity(rows, top_k, group_size)
        bf = jnp.bfloat16
        pos = jnp.where(slot_ids >= 0, expert_ids * slots + slot_ids, -1).astype(jnp.float32)
        meta = jnp.concatenate([pos.T, gate_weights.T], axis=0)
        t2, mt = comm_call(
            spread_kernel, "spread", 1, [vmem, vmem],
            [jax.ShapeDtypeStruct((4, 4, rows, width), bf), jax.ShapeDtypeStruct((3, 4, 4, 16, rows), jnp.float32)],
            [dma((2, 3))] + [dma((3, 3))] * 4 + [dma((3, 4, 2))] * 2 + [dma((3, 4, 3))] * 2 + [dma((3, 4, 2))] * 2,
        )(tokens, meta)
        s = pl.pallas_call(
            lambda *refs: pick_kernel(slots, *refs),
            name="pick",
            grid=(4, 4),
            in_specs=[pl.BlockSpec((1, 1, rows, width), lambda a, b: (a, b, 0, 0)), pl.BlockSpec((3, 1, 1, 16, rows), lambda a, b: (0, a, b, 0, 0))],
            out_specs=pl.BlockSpec((4, 2, 1, 1, slots, width), lambda a, b: (0, 0, a, b, 0, 0)),
            out_shape=jax.ShapeDtypeStruct((4, 2, 4, 4, slots, width), bf),
        )(t2, mt)
        (z5,) = comm_call(
            lambda *refs: expert_kernel(slots, *refs), "experts", 2, [hbm] * 4,
            [jax.ShapeDtypeStruct((4, 4, 2, 4, slots, width), bf)],
            [pltpu.VMEM((2, 2, 4, 4, 4, slots // 2, width), bf), pltpu.VMEM((2, 4, 2, 4, 4, slots // 2, width), bf)]
            + [pltpu.VMEM(w.shape[1:], bf) for w in (w_gate, w_up, w_down)]
            + [dma((3,)), dma((3, 2, 3))] + [dma((2, 3, 4, 2))] * 4 + [dma((2, 3, 3))] * 2,
        )(s, w_gate, w_up, w_down)
        return comm_call(
            lambda *refs: sum_kernel(slots, *refs), "weigh_sum", 4, [hbm, vmem], jax.ShapeDtypeStruct((rows, width), bf),
            [pltpu.VMEM((2, 4, 4, 2, slots, width), bf), pltpu.VMEM((4, rows, width), jnp.float32), pltpu.VMEM((3, rows, width), jnp.float32), dma((2, 3)), dma((3,)), dma((3, 3)), dma((3, 3))],
        )(z5, mt)

    return jax.shard_map(local_layer, mesh=mesh, in_specs=(tok_spec, tok_spec, tok_spec, tok_spec, weight_spec, weight_spec, weight_spec), out_specs=tok_spec, check_vma=False)
```

time: 419 us -> 341 us (0.81)
  matrix products: 55.7 us -> 0 us
  Pallas kernels: 358 us -> 336 us
    dot_general x2 -> x0, matrix products: 55.7 us -> none  [the longest x1 36.5 us: local_layer(): jnp.dot(hidden, w_down[0], preferred_element_type=jnp.float32).astype(bf)]
    pallas_call x4 -> x2, Pallas kernels: 261 us -> 239 us  [the longest x1 195 us: local_layer(): comm_call(lambda *refs: expert_kernel(slots, *refs), 'experts', 2, [hbm]...]
where the time goes in v2:
time: 341 us; the launch traced here: 340 us
  Pallas kernels  336 us (99%)
    pallas_call x1, Pallas kernels, local_layer(): comm_call(lambda *refs: expert_kernel(slots, *refs), 'experts', 2, [hbm]...  195 us
    pallas_call x1, Pallas kernels, local_layer(): comm_call(spread_kernel, 'spread', 1, [vmem, vmem], [jax.ShapeDtypeStruct...  75.6 us
    pallas_call x1, Pallas kernels, local_layer(): comm_call(lambda *refs: sum_kernel(slots, *refs), 'weigh_sum', 4, [hbm, v...  44 us
    pallas_call x1, Pallas kernels, local_layer(): pl.pallas_call(lambda *refs: pick_kernel(slots, *refs), name='pick', grid...  21.7 us

profile of v2, /device:TPU:1, one launch (start us, length us, event | category | flops | bytes accessed | tf_op | source)
XLA Modules:
  0.0 340.3 jit_solution(5179974861380479971)
XLA Ops:
  0.0 0.7 convert_bitcast_fusion
  0.7 1.3 pad_maximum_fusion.meta
  2.0 75.6 %spread.1 = (bf16[4,4,256,2048]{3,2,1,0:T(8,128)(2,1)}, f32[3,4,4,16,256]{4,3,2,1,0:T(8,128)}) custom-call(bf16[256,2048]{1,0:T(8,128)(2,1)} %tok.1, f32[16,256]{1,0:T(8,128)} %pad_maximum_fusion.meta), custom_call_target="tpu_custom_call" | custom-call | tf_op jit(solution)/shard_map/spread/pallas_call | solution.py:379
  77.6 21.7 %pick.1.refs_0_ = bf16[4,2,4,4,32,2048]{5,4,3,2,1,0:T(8,128)(2,1)} custom-call(bf16[4,4,256,2048]{3,2,1,0:T(8,128)(2,1)} %get-tuple-element.7.refs_0_, f32[3,4,4,16,256]{4,3,2,1,0:T(8,128)} %get-tuple-element.8.refs_1_), custom_call_target="tpu_custom_call" | custom-call | tf_op jit(solution)/shard_map/pick/pallas_call | solution.py:384
  99.4 194.6 %experts.1.refs_0_ = bf16[4,4,2,4,32,2048]{5,4,3,2,1,0:T(8,128)(2,1)} custom-call(bf16[4,2,4,4,32,2048]{5,4,3,2,1,0:T(8,128)(2,1)} %pick.1.refs_0_, bf16[1,2048,768]{2,1,0:T(8,128)(2,1)} %refs_1_.1, bf16[1,2048,768]{2,1,0:T(8,128)(2,1)} %refs_2_.1, bf16[1,768,2048]{2,1,0:T(8,128)(2,1)} %refs_3_.1), custom_call_target="tpu_custom_call" | custom-call | tf_op jit(solution)/shard_map/experts/pallas_call | solution.py:392
  294.0 44.0 %weigh_sum.1 = bf16[256,2048]{1,0:T(8,128)(2,1)} custom-call(bf16[4,4,2,4,32,2048]{5,4,3,2,1,0:T(8,128)(2,1)} %experts.1.refs_0_, f32[3,4,4,16,256]{4,3,2,1,0:T(8,128)} %get-tuple-element.8.refs_1_), custom_call_target="tpu_custom_call" | custom-call | tf_op jit(solution)/shard_map/weigh_sum/pallas_call | solution.py:399
  338.0 2.3 copy.9

commit v3 on v2

--- a/solution.py
+++ b/solution.py
@@ -71,94 +71,133 @@
     return out
 
 
-def spread_kernel(tok, meta, t2, mt, loc, s1s, s1r, m1s, m1r, s2s, s2r, m2s, m2r, s3s, s3r):
+def spread_kernel(slots, tok, meta, s_ref, mt, t2, tile0, tile1, tile2, loc, out_sem, s1s, s1r, m1s, m1r, s2s, s2r, m2s, m2r, s3s, s3r):
     core, e, views = place()
     v, st = own_view(core, views)
     greet(ring_peers((core,), e, views))
-    half = tok.shape[0] // 2
-    sends, locals_ = [], []
-
-    def go(copy):
-        copy.start()
-        sends.append(copy)
+    rows = tok.shape[0]
+    tiles = (tile0, tile1, tile2)
+
+    def at(k, j0, j1):
+        i0, i1, _ = dims(k)
+        return plane_at(k, lax.rem(v[i0] + j0, RING), lax.rem(v[i1] + j1, RING))
+
+    def block(k, j0, j1):
+        return t2.at[(*at(k, j0, j1), slice(None), cols(k))]
+
+    def info(k, j0, j1):
+        return mt.at[(k, *at(k, j0, j1))]
+
+    def first(k, delta):
+        i0 = dims(k)[0]
+        peer = step(e, v[i0], st[i0], delta)
+        return (remote(tok.at[:, cols(k)], block(k, 0, 0), s1s.at[k, delta - 1], s1r.at[k, delta - 1], core, peer),
+                remote(meta, info(k, 0, 0), m1s.at[k, delta - 1], m1r.at[k, delta - 1], core, peer))
+
+    def second(k, j, way):
+        i1 = dims(k)[1]
+        return remote(block(k, j, 0), block(k, j, 0), s2s.at[k, j, way], s2r.at[k, j, way], core, step(e, v[i1], st[i1], 1 + 2 * way))
+
+    def second_info(k, j, delta):
+        i1 = dims(k)[1]
+        return remote(info(k, j, 0), info(k, j, 0), m2s.at[k, j, delta - 1], m2r.at[k, j, delta - 1], core, step(e, v[i1], st[i1], delta))
+
+    def third(k, j, way):
+        i1 = dims(k)[1]
+        piece = t2.at[(*at(k, j, 3 - 2 * way), pl.ds(rows // 2 * way, rows // 2), cols(k))]
+        return remote(piece, piece, s3s.at[k, j, way], s3r.at[k, j, way], core, step(e, v[i1], st[i1], 1 + 2 * way))
+
+    def second_all(k, j):
+        for way in range(2):
+            second(k, j, way).start()
+        for delta in DELTAS:
+            second_info(k, j, delta).start()
+
+    def keep(k):
+        return pltpu.make_async_copy(tok.at[:, cols(k)], block(k, 0, 0), loc.at[0, k]), pltpu.make_async_copy(meta, info(k, 0, 0), loc.at[1, k])
+
+    def put(k, n, j0, j1):
+        return pltpu.make_async_copy(tiles[k].at[lax.rem(n, 2)], s_ref.at[(slice(None), slice(None), *at(k, j0, j1), slice(None), cols(k))], out_sem.at[k, lax.rem(n, 2)])
+
+    def pick(k, n, j0, j1):
+        i0, i1, i2 = dims(k)
+        total = RING * 2 * slots
+        r = lax.broadcasted_iota(jnp.int32, (total, 1), 0)
+        p2, half, s = r // (2 * slots), (r // slots) % 2, r % slots
+        key = ((half * 64 + v[i0] * st[i0] + v[i1] * st[i1] + p2 * st[i2]) * slots + s).astype(jnp.float32)
+        a, b = at(k, j0, j1)
+        hot = jnp.zeros((total, rows), jnp.float32)
+        for j in range(8):
+            hot = jnp.where(key == mt[k, a, b, j:j + 1, :], 1.0, hot)
+        got = jnp.dot(hot.astype(jnp.bfloat16), t2[a, b, :, cols(k)], preferred_element_type=jnp.float32)
+
+        @pl.when(n >= 2)
+        def _():
+            put(k, n, j0, j1).wait()
+
+        tiles[k][lax.rem(n, 2)] = got.astype(jnp.bfloat16).reshape(RING, 2, slots, COLS[k][1])
+        put(k, n, j0, j1).start()
+
+    def gray(t):
+        return t + (t // 2) * (5 - 2 * t)
 
     for k in range(3):
-        i0, i1, _ = dims(k)
-        here = plane_at(k, v[i0], v[i1])
+        for copy in keep(k):
+            copy.start()
+    for delta in (2, 1, 3):
+        for k in range(3):
+            for copy in first(k, delta):
+                copy.start()
+    for k in range(3):
+        for copy in keep(k):
+            copy.wait()
+        second_all(k, 0)
+    for j in DELTAS:
+        for k in range(3):
+            remote(block(k, j, 0), block(k, j, 0), s1s.at[k, 3 - j], s1r.at[k, 3 - j], core, e).wait_recv()
+            remote(info(k, j, 0), info(k, j, 0), m1s.at[k, 3 - j], m1r.at[k, 3 - j], core, e).wait_recv()
+            second_all(k, j)
+
+    @pl.loop(0, RING)
+    def _(t):
+        j = gray(t)
+        for k in range(3):
+            for way in range(2):
+                came = block(k, j, 3 - 2 * way)
+                remote(came, came, s2s.at[k, j, way], s2r.at[k, j, way], core, e).wait_recv()
+                third(k, j, way).start()
+            for delta in (1, 3):
+                came = info(k, j, 4 - delta)
+                remote(came, came, m2s.at[k, j, delta - 1], m2r.at[k, j, delta - 1], core, e).wait_recv()
+
+        @pl.loop(0, 3)
+        def _(d):
+            for k in range(3):
+                pick(k, t * 3 + d, j, d + d // 2)
+
+    @pl.loop(0, RING)
+    def _(t):
+        j = gray(t)
+        for k in range(3):
+            for way in range(2):
+                came = t2.at[(*at(k, j, 2), pl.ds(rows // 2 * way, rows // 2), cols(k))]
+                remote(came, came, s3s.at[k, j, way], s3r.at[k, j, way], core, e).wait_recv()
+            came = info(k, j, 2)
+            remote(came, came, m2s.at[k, j, 1], m2r.at[k, j, 1], core, e).wait_recv()
+            pick(k, 12 + t, j, 2)
+
+    for k in range(3):
+        for n in range(2):
+            put(k, n, 0, 0).wait()
         for delta in DELTAS:
-            peer = step(e, v[i0], st[i0], delta)
-            go(remote(tok.at[:, cols(k)], t2.at[(*here, slice(None), cols(k))], s1s.at[k, delta - 1], s1r.at[k, delta - 1], core, peer))
-            go(remote(meta, mt.at[(k, *here)], m1s.at[k, delta - 1], m1r.at[k, delta - 1], core, peer))
-    for k in range(3):
-        i0, i1, _ = dims(k)
-        here = plane_at(k, v[i0], v[i1])
-        own = pltpu.make_async_copy(tok.at[:, cols(k)], t2.at[(*here, slice(None), cols(k))], loc.at[0, k])
-        own.start()
-        locals_.append(own)
-        own = pltpu.make_async_copy(meta, mt.at[(k, *here)], loc.at[1, k])
-        own.start()
-        locals_.append(own)
-
-    def second(k, j):
-        i0, i1, _ = dims(k)
-        at = plane_at(k, lax.rem(v[i0] + j, RING), v[i1])
-        block = t2.at[(*at, slice(None), cols(k))]
-        for way, delta in enumerate((1, 3)):
-            src = tok.at[:, cols(k)] if j == 0 else block
-            go(remote(src, block, s2s.at[k, j, way], s2r.at[k, j, way], core, step(e, v[i1], st[i1], delta)))
-        for delta in DELTAS:
-            src = meta if j == 0 else mt.at[(k, *at)]
-            go(remote(src, mt.at[(k, *at)], m2s.at[k, j, delta - 1], m2r.at[k, j, delta - 1], core, step(e, v[i1], st[i1], delta)))
-
-    for k in range(3):
-        second(k, 0)
-    for j in DELTAS:
-        for k in range(3):
-            i0, i1, _ = dims(k)
-            at = plane_at(k, lax.rem(v[i0] + j, RING), v[i1])
-            block = t2.at[(*at, slice(None), cols(k))]
-            remote(block, block, s1s.at[k, 3 - j], s1r.at[k, 3 - j], core, e).wait_recv()
-            remote(mt.at[(k, *at)], mt.at[(k, *at)], m1s.at[k, 3 - j], m1r.at[k, 3 - j], core, e).wait_recv()
-            second(k, j)
-    for j in (0, *DELTAS):
-        for k in range(3):
-            i0, i1, _ = dims(k)
-            for way, delta in enumerate((1, 3)):
-                at = plane_at(k, lax.rem(v[i0] + j, RING), lax.rem(v[i1] + 4 - delta, RING))
-                block = t2.at[(*at, slice(None), cols(k))]
-                remote(block, block, s2s.at[k, j, way], s2r.at[k, j, way], core, e).wait_recv()
-                part = t2.at[(*at, pl.ds(half * way, half), cols(k))]
-                go(remote(part, part, s3s.at[k, j, way], s3r.at[k, j, way], core, step(e, v[i1], st[i1], delta)))
-    for j in (0, *DELTAS):
-        for k in range(3):
-            i0, i1, _ = dims(k)
-            for delta in DELTAS:
-                at = plane_at(k, lax.rem(v[i0] + j, RING), lax.rem(v[i1] + 4 - delta, RING))
-                remote(mt.at[(k, *at)], mt.at[(k, *at)], m2s.at[k, j, delta - 1], m2r.at[k, j, delta - 1], core, e).wait_recv()
-            at = plane_at(k, lax.rem(v[i0] + j, RING), lax.rem(v[i1] + 2, RING))
+            for copy in first(k, delta):
+                copy.wait_send()
+        for j in range(RING):
             for way in range(2):
-                part = t2.at[(*at, pl.ds(half * way, half), cols(k))]
-                remote(part, part, s3s.at[k, j, way], s3r.at[k, j, way], core, e).wait_recv()
-    for copy in sends:
-        copy.wait_send()
-    for copy in locals_:
-        copy.wait()
-
-
-def pick_kernel(slots, t2, mt, out):
-    core, e, views = place()
-    v, st = own_view(core, views)
-    rows = RING * 2 * slots
-    r = lax.broadcasted_iota(jnp.int32, (rows, 1), 0)
-    p2, half, s = r // (2 * slots), (r // slots) % 2, r % slots
-    for k in range(3):
-        i0, i1, i2 = dims(k)
-        key = ((half * 64 + v[i0] * st[i0] + v[i1] * st[i1] + p2 * st[i2]) * slots + s).astype(jnp.float32)
-        hot = jnp.zeros((rows, t2.shape[2]), jnp.float32)
-        for j in range(8):
-            hot = jnp.where(key == mt[k, 0, 0, j:j + 1, :], 1.0, hot)
-        got = jnp.dot(hot.astype(jnp.bfloat16), t2[0, 0, :, cols(k)], preferred_element_type=jnp.float32)
-        out[:, :, 0, 0, :, cols(k)] = got.astype(jnp.bfloat16).reshape(RING, 2, slots, COLS[k][1])
+                second(k, j, way).wait_send()
+                third(k, j, way).wait_send()
+            for delta in DELTAS:
+                second_info(k, j, delta).wait_send()
 
 
 def expert_kernel(slots, s_ref, wg_ref, wu_ref, wd_ref, z5, r, z4, wg, wu, wd, wsem, loc, s3, r3, s4, r4, s5, r5):
@@ -376,19 +415,16 @@
         bf = jnp.bfloat16
         pos = jnp.where(slot_ids >= 0, expert_ids * slots + slot_ids, -1).astype(jnp.float32)
         meta = jnp.concatenate([pos.T, gate_weights.T], axis=0)
-        t2, mt = comm_call(
-            spread_kernel, "spread", 1, [vmem, vmem],
-            [jax.ShapeDtypeStruct((4, 4, rows, width), bf), jax.ShapeDtypeStruct((3, 4, 4, 16, rows), jnp.float32)],
-            [dma((2, 3))] + [dma((3, 3))] * 4 + [dma((3, 4, 2))] * 2 + [dma((3, 4, 3))] * 2 + [dma((3, 4, 2))] * 2,
+        s, mt = pl.pallas_call(
+            lambda *refs: spread_kernel(slots, *refs),
+            name="spread",
+            in_specs=[vmem, vmem],
+            out_specs=[hbm, vmem],
+            out_shape=[jax.ShapeDtypeStruct((4, 2, 4, 4, slots, width), bf), jax.ShapeDtypeStruct((3, 4, 4, 16, rows), jnp.float32)],
+            scratch_shapes=[pltpu.VMEM((4, 4, rows, width), bf)] + [pltpu.VMEM((2, 4, 2, slots, n), bf) for _, n in COLS]
+            + [dma((2, 3)), dma((3, 2))] + [dma((3, 3))] * 4 + [dma((3, 4, 2))] * 2 + [dma((3, 4, 3))] * 2 + [dma((3, 4, 2))] * 2,
+            compiler_params=pltpu.CompilerParams(collective_id=1, has_side_effects=True),
         )(tokens, meta)
-        s = pl.pallas_call(
-            lambda *refs: pick_kernel(slots, *refs),
-            name="pick",
-            grid=(4, 4),
-            in_specs=[pl.BlockSpec((1, 1, rows, width), lambda a, b: (a, b, 0, 0)), pl.BlockSpec((3, 1, 1, 16, rows), lambda a, b: (0, a, b, 0, 0))],
-            out_specs=pl.BlockSpec((4, 2, 1, 1, slots, width), lambda a, b: (0, 0, a, b, 0, 0)),
-            out_shape=jax.ShapeDtypeStruct((4, 2, 4, 4, slots, width), bf),
-        )(t2, mt)
         (z5,) = comm_call(
             lambda *refs: expert_kernel(slots, *refs), "experts", 2, [hbm] * 4,
             [jax.ShapeDtypeStruct((4, 4, 2, 4, slots, width), bf)],

time: 341 us -> 322 us (0.944)
  Pallas kernels: 336 us -> 317 us
    pallas_call x2 -> x1, Pallas kernels: 97.3 us -> 78.3 us  [local_layer(): pl.pallas_call(lambda *refs: spread_kernel(slots, *refs), name='spread',...]
where the time goes in v3:
time: 322 us; the launch traced here: 321 us
  Pallas kernels  317 us (98%)
    pallas_call x1, Pallas kernels, local_layer(): comm_call(lambda *refs: expert_kernel(slots, *refs), 'experts', 2, [hbm]...  195 us
    pallas_call x1, Pallas kernels, local_layer(): pl.pallas_call(lambda *refs: spread_kernel(slots, *refs), name='spread',...  78.3 us
    pallas_call x1, Pallas kernels, local_layer(): comm_call(lambda *refs: sum_kernel(slots, *refs), 'weigh_sum', 4, [hbm, v...  43.8 us

profile of v3, /device:TPU:1, one launch (start us, length us, event | category | flops | bytes accessed | tf_op | source)
XLA Modules:
  0.0 321.5 jit_solution(15621198910768599955)
XLA Ops:
  0.0 0.7 convert_bitcast_fusion
  0.7 1.3 pad_maximum_fusion.refs_1_
  2.0 78.3 %spread.1 = (bf16[4,2,4,4,32,2048]{5,4,3,2,1,0:T(8,128)(2,1)}, f32[3,4,4,16,256]{4,3,2,1,0:T(8,128)}) custom-call(bf16[256,2048]{1,0:T(8,128)(2,1)} %refs_0_.1, f32[16,256]{1,0:T(8,128)} %pad_maximum_fusion.refs_1_), custom_call_target="tpu_custom_call" | custom-call | tf_op jit(solution)/shard_map/spread/pallas_call | solution.py:418
  80.3 195.1 %experts.1.refs_0_ = bf16[4,4,2,4,32,2048]{5,4,3,2,1,0:T(8,128)(2,1)} custom-call(bf16[4,2,4,4,32,2048]{5,4,3,2,1,0:T(8,128)(2,1)} %get-tuple-element.7.refs_0_, bf16[1,2048,768]{2,1,0:T(8,128)(2,1)} %refs_1_.1, bf16[1,2048,768]{2,1,0:T(8,128)(2,1)} %refs_2_.1, bf16[1,768,2048]{2,1,0:T(8,128)(2,1)} %refs_3_.1), custom_call_target="tpu_custom_call" | custom-call | tf_op jit(solution)/shard_map/experts/pallas_call | solution.py:428
  275.4 43.8 %weigh_sum.1 = bf16[256,2048]{1,0:T(8,128)(2,1)} custom-call(bf16[4,4,2,4,32,2048]{5,4,3,2,1,0:T(8,128)(2,1)} %experts.1.refs_0_, f32[3,4,4,16,256]{4,3,2,1,0:T(8,128)} %get-tuple-element.8.refs_1_), custom_call_target="tpu_custom_call" | custom-call | tf_op jit(solution)/shard_map/weigh_sum/pallas_call | solution.py:435
  319.2 2.3 copy.9

commit v4 on v3

v4 whole, which is shorter than its diff:
```python
import jax
import jax.numpy as jnp
from jax import lax
from jax.experimental import pallas as pl
from jax.experimental.pallas import tpu as pltpu
from jax.sharding import PartitionSpec as P

MESH = pl.DeviceIdType.MESH
CAP_FACTOR = 2
RING = 4
DELTAS = (1, 3, 2)
COLS = ((0, 768), (768, 640), (1408, 640))
STRIDES = ((16, 4, 1), (4, 1, 16))


def capacity(rows, top_k, experts):
    return ((CAP_FACTOR * rows * top_k + 8 * experts - 1) // (8 * experts)) * 8


def place():
    core, e = lax.axis_index("node"), lax.axis_index("expert")
    z, y, x = e // 16, (e // 4) % 4, e % 4
    return core, e, ((z, y, x), (y, x, z))


def own_view(core, views):
    v = tuple(a + core * (b - a) for a, b in zip(*views))
    s = tuple(a + core * (b - a) for a, b in zip(*STRIDES))
    return v, s


def step(e, pos, stride, delta):
    return e + (lax.rem(pos + delta, RING) - pos) * stride


def cols(k):
    return pl.ds(*COLS[k])


def dims(k):
    return k % 3, (k + 1) % 3, (k + 2) % 3


def plane_at(k, d0, d1):
    return (d1, d0) if k == 2 else (d0, d1)


def cube_at(k, p):
    full = [slice(None)] * 3
    full[dims(k)[2]] = p
    return tuple(full)


def remote(src, dst, send, recv, core, e):
    return pltpu.make_async_remote_copy(src_ref=src, dst_ref=dst, send_sem=send, recv_sem=recv, device_id=(0, core, e), device_id_type=MESH)


def greet(targets):
    barrier = pltpu.get_barrier_semaphore()
    for core, e in targets:
        pl.semaphore_signal(barrier, inc=1, device_id=(0, core, e), device_id_type=MESH)
    pl.semaphore_wait(barrier, len(targets))


def ring_peers(core_list, e, views):
    out = []
    for core in core_list:
        for v, s in zip(views[0], STRIDES[0]):
            for delta in DELTAS:
                out.append((core, step(e, v, s, delta)))
    return out


def layer_kernel(slots, tok, meta, wg_ref, wu_ref, wd_ref, s_ref, z4, z5, own, came2, mt, t2, tile0, tile1, tile2, r, bounce, wg, wu, wd, sums, passing,
                 loc0, out_sem, s1s, s1r, m1s, m1r, s2s, s2r, m2s, m2r, s3s, s3r, wsem, loc, xes, xer, xs, xr, s4, r4, s5, r5,
                 relay_s, relay_r, load_sem, hs, hr, ps, pr):
    core, e, views = place()
    v, st = own_view(core, views)
    other = own_view(1 - core, views)[0]
    half_slots = slots // 2
    loads = [pltpu.make_async_copy(src.at[0], dst, wsem.at[i]) for i, (src, dst) in enumerate(((wg_ref, wg), (wu_ref, wu), (wd_ref, wd)))]
    greet(ring_peers((0, 1), e, views) + [(1 - core, e)])
    rows = tok.shape[0]
    tiles = (tile0, tile1, tile2)

    def at(k, j0, j1):
        i0, i1, _ = dims(k)
        return plane_at(k, lax.rem(v[i0] + j0, RING), lax.rem(v[i1] + j1, RING))

    def block(k, j0, j1):
        return t2.at[(*at(k, j0, j1), slice(None), cols(k))]

    def info(k, j0, j1):
        return mt.at[(k, *at(k, j0, j1))]

    def first(k, delta):
        i0 = dims(k)[0]
        return remote(tok.at[:, cols(k)], block(k, 0, 0), s1s.at[k, delta - 1], s1r.at[k, delta - 1], core, step(e, v[i0], st[i0], delta))

    def first_info(k, delta):
        i0 = dims(k)[0]
        return remote(meta, info(k, 0, 0), m1s.at[k, delta - 1], m1r.at[k, delta - 1], core, step(e, v[i0], st[i0], delta))

    def relay(k, way):
        i0 = dims(k)[0]
        piece = t2.at[(*at(k, 3 - 2 * way, 0), pl.ds(rows // 2 * way, rows // 2), cols(k))]
        return remote(piece, piece, relay_s.at[k, way], relay_r.at[k, way], core, step(e, v[i0], st[i0], 1 + 2 * way))

    def second(k, j, way):
        i1 = dims(k)[1]
        return remote(block(k, j, 0), block(k, j, 0), s2s.at[k, j, way], s2r.at[k, j, way], core, step(e, v[i1], st[i1], 1 + 2 * way))

    def second_info(k, j, delta):
        i1 = dims(k)[1]
        return remote(info(k, j, 0), info(k, j, 0), m2s.at[k, j, delta - 1], m2r.at[k, j, delta - 1], core, step(e, v[i1], st[i1], delta))

    def third(k, j, way):
        i1 = dims(k)[1]
        piece = t2.at[(*at(k, j, 3 - 2 * way), pl.ds(rows // 2 * way, rows // 2), cols(k))]
        return remote(piece, piece, s3s.at[k, j, way], s3r.at[k, j, way], core, step(e, v[i1], st[i1], 1 + 2 * way))

    def second_all(k, j):
        for way in range(2):
            second(k, j, way).start()
        for delta in DELTAS:
            second_info(k, j, delta).start()

    def keep(k):
        return pltpu.make_async_copy(tok.at[:, cols(k)], block(k, 0, 0), loc0.at[0, k]), pltpu.make_async_copy(meta, info(k, 0, 0), loc0.at[1, k])

    def put(k, n, j0, j1):
        return pltpu.make_async_copy(tiles[k].at[lax.rem(n, 2)], s_ref.at[(slice(None), slice(None), *at(k, j0, j1), slice(None), cols(k))], out_sem.at[k, lax.rem(n, 2)])

    def pick(k, n, j0, j1):
        i0, i1, i2 = dims(k)
        total = RING * 2 * slots
        r = lax.broadcasted_iota(jnp.int32, (total, 1), 0)
        p2, half, s = r // (2 * slots), (r // slots) % 2, r % slots
        key = ((half * 64 + v[i0] * st[i0] + v[i1] * st[i1] + p2 * st[i2]) * slots + s).astype(jnp.float32)
        a, b = at(k, j0, j1)
        hot = jnp.zeros((total, rows), jnp.float32)
        for j in range(8):
            hot = jnp.where(key == mt[k, a, b, j:j + 1, :], 1.0, hot)
        got = jnp.dot(hot.astype(jnp.bfloat16), t2[a, b, :, cols(k)], preferred_element_type=jnp.float32)

        @pl.when(n >= 2)
        def _():
            put(k, n, j0, j1).wait()

        tiles[k][lax.rem(n, 2)] = got.astype(jnp.bfloat16).reshape(RING, 2, slots, COLS[k][1])
        put(k, n, j0, j1).start()

    def gray(t):
        return t + (t // 2) * (5 - 2 * t)

    for k in range(3):
        for copy in keep(k):
            copy.start()
    for delta in DELTAS:
        for k in range(3):
            if delta != 2:
                first(k, delta).start()
            first_info(k, delta).start()
    for k in range(3):
        for copy in keep(k):
            copy.wait()
        second_all(k, 0)
    for j in DELTAS:
        for k in range(3):
            if j == 2:
                for way in range(2):
                    piece = t2.at[(*at(k, 2, 0), pl.ds(rows // 2 * way, rows // 2), cols(k))]
                    remote(piece, piece, relay_s.at[k, way], relay_r.at[k, way], core, e).wait_recv()
            else:
                remote(block(k, j, 0), block(k, j, 0), s1s.at[k, 3 - j], s1r.at[k, 3 - j], core, e).wait_recv()
                relay(k, (3 - j) // 2).start()
            remote(info(k, j, 0), info(k, j, 0), m1s.at[k, 3 - j], m1r.at[k, 3 - j], core, e).wait_recv()
            second_all(k, j)

    @pl.loop(0, RING)
    def _(t):
        j = gray(t)
        for k in range(3):
            for way in range(2):
                came = block(k, j, 3 - 2 * way)
                remote(came, came, s2s.at[k, j, way], s2r.at[k, j, way], core, e).wait_recv()
                third(k, j, way).start()
            for delta in (1, 3):
                came = info(k, j, 4 - delta)
                remote(came, came, m2s.at[k, j, delta - 1], m2r.at[k, j, delta - 1], core, e).wait_recv()

        @pl.loop(0, 3)
        def _(d):
            for k in range(3):
                pick(k, t * 3 + d, j, d + d // 2)

    for k in range(3):
        for n in range(2):
            put(k, n, 0, 0).wait()

    def span(q):
        return pl.ds(half_slots * q, half_slots)

    def cube(q, o, k, p):
        return r.at[(q, o, *cube_at(k, p), slice(None), cols(k))]

    def rod(q, o, k, p, d1):
        at = list(cube_at(k, p))
        at[dims(k)[1]] = d1
        return r.at[(q, o, *at, slice(None), cols(k))]

    def rod_out(q, k, p, d1, to):
        at = (d1, slice(None)) if k == 2 else (slice(None), d1)
        return s_ref.at[(p, to, *at, span(q), cols(k))]

    def early(k, j1, delta, to):
        i1, i2 = dims(k)[1:]
        d1 = lax.rem(v[i1] + j1, RING)
        return remote(rod_out(0, k, lax.rem(v[i2] + delta, RING), d1, to), rod(0, core, k, v[i2], d1), xes.at[k, j1, delta, to], xer.at[k, j1, delta, core], to, step(e, v[i2], st[i2], delta))

    def late(k, delta, to):
        i2 = dims(k)[2]
        return remote(s_ref.at[lax.rem(v[i2] + delta, RING), to, :, :, span(1), cols(k)], cube(1, core, k, v[i2]), xs.at[1, k, delta, to], xr.at[1, k, delta, core], to, step(e, v[i2], st[i2], delta))

    def beside(q, k):
        i2 = dims(k)[2]
        return remote(s_ref.at[v[i2], 1 - core, :, :, span(q), cols(k)], cube(q, core, k, v[i2]), xs.at[q, k, 0, 0], xr.at[q, k, 0, 0], 1 - core, e)

    def inward(q, k):
        i2 = dims(k)[2]
        return pltpu.make_async_copy(s_ref.at[v[i2], core, :, :, span(q), cols(k)], cube(q, core, k, v[i2]), loc.at[0, q, k])


    @pl.loop(0, 3)
    def _(d):
        for delta in DELTAS:
            for k in range(3):
                for to in range(2):
                    early(k, d + d // 2, delta, to).start()

    for load in loads:
        load.start()

    @pl.loop(0, RING)
    def _(t):
        j = gray(t)
        for k in range(3):
            for way in range(2):
                came = t2.at[(*at(k, j, 2), pl.ds(rows // 2 * way, rows // 2), cols(k))]
                remote(came, came, s3s.at[k, j, way], s3r.at[k, j, way], core, e).wait_recv()
            came = info(k, j, 2)
            remote(came, came, m2s.at[k, j, 1], m2r.at[k, j, 1], core, e).wait_recv()
            pick(k, t, j, 2)

    for k in range(3):
        for n in range(2):
            put(k, n, 0, 0).wait()
    for delta in DELTAS:
        for k in range(3):
            for to in range(2):
                early(k, 2, delta, to).start()
    for q in range(2):
        for k in range(3):
            beside(q, k).start()
            inward(q, k).start()
    for delta in DELTAS:
        for k in range(3):
            for to in range(2):
                late(k, delta, to).start()
    for load in loads:
        load.wait()

    def z4_at(q, k, p, c):
        return z4.at[q, p, c, :, :, :, cols(k)]

    def back(q, o, k, delta):
        i2 = dims(k)[2]
        here = views[o][i2]
        return remote(cube(q, o, k, lax.rem(here + delta, RING)), z4_at(q, k, here, core), s4.at[q, k, delta, o], r4.at[q, k, delta, core], o, step(e, here, STRIDES[o][i2], delta))

    def across(q, k):
        i2 = dims(k)[2]
        return remote(cube(q, 1 - core, k, other[i2]), z4_at(q, k, other[i2], core), s4.at[q, k, 0, 0], r4.at[q, k, 0, 0], 1 - core, e)

    def stay(q, k):
        i2 = dims(k)[2]
        return pltpu.make_async_copy(cube(q, core, k, v[i2]), z4_at(q, k, v[i2], core), loc.at[1, q, k])

    @pl.loop(0, 2)
    def _(q):
        for k in range(3):
            i1, i2 = dims(k)[1:]
            inward(q, k).wait()
            target = cube(q, 1 - core, k, other[i2])
            remote(target, target, xs.at[q, k, 0, 0], xr.at[q, k, 0, 0], core, e).wait_recv()

        @pl.when(q == 0)
        def _():
            @pl.loop(0, RING)
            def _(j1):
                for k in range(3):
                    i1, i2 = dims(k)[1:]
                    for delta in DELTAS:
                        for o in range(2):
                            target = rod(0, o, k, lax.rem(views[o][i2] + 4 - delta, RING), lax.rem(views[o][i1] + j1, RING))
                            remote(target, target, xes.at[k, j1, delta, 0], xer.at[k, j1, delta, o], core, e).wait_recv()

        @pl.when(q == 1)
        def _():
            for k in range(3):
                i2 = dims(k)[2]
                for delta in DELTAS:
                    for o in range(2):
                        target = cube(1, o, k, lax.rem(views[o][i2] + 4 - delta, RING))
                        remote(target, target, xs.at[1, k, delta, 0], xr.at[1, k, delta, o], core, e).wait_recv()

        for o in range(2):
            @pl.loop(0, RING)
            def _(i):
                x = r[q, o, i].reshape(RING * RING * half_slots, r.shape[-1])
                gate = jnp.dot(x, wg[...], preferred_element_type=jnp.float32)
                up = jnp.dot(x, wu[...], preferred_element_type=jnp.float32)
                hidden = (jax.nn.silu(gate) * up).astype(jnp.bfloat16)
                y = jnp.dot(hidden, wd[...], preferred_element_type=jnp.float32).astype(jnp.bfloat16)
                r[q, o, i] = y.reshape(RING, RING, half_slots, r.shape[-1])

            for delta in DELTAS:
                for k in range(3):
                    back(q, o, k, delta).start()
        for k in range(3):
            across(q, k).start()
            stay(q, k).start()

    def line(q, k, p):
        at = (slice(None), slice(None), p, slice(None)) if k == 2 else (slice(None), slice(None), slice(None), p)
        return z4.at[(q, *at, slice(None), cols(k))]

    def forth(q, k, delta):
        i1 = dims(k)[1]
        return remote(line(q, k, lax.rem(v[i1] + delta, RING)), z5.at[v[i1], :, :, :, span(q), cols(k)], s5.at[q, k, delta - 1], r5.at[q, k, delta - 1], core, step(e, v[i1], st[i1], delta))

    def lift(q, k, stage):
        i1 = dims(k)[1]
        room = bounce.at[q, :, :, :, :, cols(k)]
        if stage == 0:
            return pltpu.make_async_copy(line(q, k, v[i1]), room, loc.at[2, q, k])
        return pltpu.make_async_copy(room, z5.at[v[i1], :, :, :, span(q), cols(k)], loc.at[3, q, k])

    for q in range(2):
        for k in range(3):
            i2 = dims(k)[2]
            stay(q, k).wait()
            target = z4_at(q, k, v[i2], 1 - core)
            remote(target, target, s4.at[q, k, 0, 0], r4.at[q, k, 0, 0], core, e).wait_recv()
            for delta in DELTAS:
                for o in range(2):
                    target = z4_at(q, k, lax.rem(v[i2] + 4 - delta, RING), o)
                    remote(target, target, s4.at[q, k, delta, 0], r4.at[q, k, delta, o], core, e).wait_recv()
            for delta in DELTAS:
                forth(q, k, delta).start()
            lift(q, k, 0).start()
        for k in range(3):
            lift(q, k, 0).wait()
            lift(q, k, 1).start()
    @pl.loop(0, RING)
    def _(j):
        for k in range(3):
            for way in range(2):
                second(k, j, way).wait_send()
                third(k, j, way).wait_send()

    for k in range(3):
        for way in range(2):
            relay(k, way).wait_send()

    def fetch(q, turn, k, c):
        d0 = lax.rem(v[dims(k)[0]] + RING - turn + 2, RING)
        return pltpu.make_async_copy(z5.at[:, :, c, d0, span(q), cols(k)], t2.at[:, :, pl.ds(32 * (RING * q + turn) + half_slots * c, half_slots), cols(k)], load_sem.at[q, turn, k, c])

    def near(k, delta, part):
        i0 = dims(k)[0]
        at = pl.ds(rows // 2 * part, rows // 2)
        way = delta // 2
        return remote(sums.at[delta, at, cols(k)], came2.at[way, at, cols(k)], ps.at[k, way, part], pr.at[k, way, part], core, step(e, v[i0], st[i0], delta))

    def far(k, way):
        i0 = dims(k)[0]
        at = pl.ds(rows // 2 * way, rows // 2)
        return remote(sums.at[2, at, cols(k)], passing.at[way, :, cols(k)], hs.at[k, way], hr.at[k, way], core, step(e, v[i0], st[i0], 1 + 2 * way))

    def join(k, delta):
        way = delta // 2
        at = pl.ds(rows // 2 * way, rows // 2)
        remote(passing.at[way, :, cols(k)], passing.at[way, :, cols(k)], hs.at[k, way], hr.at[k, way], core, e).wait_recv()
        sums[delta, at, cols(k)] += passing[way, :, cols(k)]
        near(k, delta, way).start()

    n = RING * RING * 2 * half_slots
    lane = lax.broadcasted_iota(jnp.int32, (1, n), 1)
    place_of = (lane // (RING * 2 * half_slots), (lane // (2 * half_slots)) % RING, (lane // half_slots) % 2, lane % half_slots)

    def weigh(q, turn, delta, k):
        d1, p2, half, s = place_of
        i0, i1, i2 = dims(k)
        for c in range(2):
            fetch(q, turn, k, c).wait()
        a, b = at(k, delta, 0)
        m = jnp.transpose(mt[k, a, b])
        key = ((half * 64 + v[i0] * st[i0] + d1 * st[i1] + p2 * st[i2]) * slots + half_slots * q + s).astype(jnp.float32)
        w = jnp.zeros((rows, n), jnp.float32)
        for j in range(8):
            w = jnp.where(m[:, j:j + 1] == key, m[:, 8 + j:9 + j], w)
        hi = w.astype(jnp.bfloat16)
        rest = w - hi.astype(jnp.float32)
        mid = rest.astype(jnp.bfloat16)
        low = (rest - mid.astype(jnp.float32)).astype(jnp.bfloat16)
        y = t2[:, :, pl.ds(32 * (RING * q + turn), 32), cols(k)].reshape(n, COLS[k][1])
        total = jnp.dot(low, y, preferred_element_type=jnp.float32)
        total += jnp.dot(mid, y, preferred_element_type=jnp.float32)
        total += jnp.dot(hi, y, preferred_element_type=jnp.float32)
        if q == 0:
            sums[delta, :, cols(k)] = total
        else:
            sums[delta, :, cols(k)] += total

    def turn_delta(turn):
        return lax.rem(RING - turn + 2, RING)

    for q in range(2):
        for k in range(3):
            lift(q, k, 1).wait()
            i1 = dims(k)[1]
            for delta in DELTAS:
                target = z5.at[lax.rem(v[i1] + 4 - delta, RING), :, :, :, span(q), cols(k)]
                remote(target, target, s5.at[q, k, delta - 1], r5.at[q, k, delta - 1], core, e).wait_recv()
            for turn in range(RING):
                for c in range(2):
                    fetch(q, turn, k, c).start()

        @pl.loop(0, RING)
        def _(turn):
            for k in range(3):
                delta = turn_delta(turn)
                weigh(q, turn, delta, k)
                if q == 1:
                    @pl.when(turn == 0)
                    def _():
                        for way in range(2):
                            far(k, way).start()

                    @pl.when(turn == 1)
                    def _():
                        near(k, 1, 1).start()

                    @pl.when(turn == 3)
                    def _():
                        near(k, 3, 0).start()

            if q == 1:
                @pl.when(turn == 2)
                def _():
                    for k in range(3):
                        join(k, 1)

    for k in range(3):
        join(k, 3)
    keep = pltpu.make_async_copy(sums.at[0], own, load_sem.at[0, 0, 0, 0])
    keep.start()
    for k in range(3):
        for way in range(2):
            for part in range(2):
                target = came2.at[way, pl.ds(rows // 2 * part, rows // 2), cols(k)]
                remote(target, target, ps.at[k, way, part], pr.at[k, way, part], core, e).wait_recv()
    keep.wait()

    @pl.loop(0, RING)
    def _(j):
        for k in range(3):
            for delta in DELTAS:
                second_info(k, j, delta).wait_send()
                for to in range(2):
                    early(k, j, delta, to).wait_send()

    for k in range(3):
        for delta in DELTAS:
            if delta != 2:
                first(k, delta).wait_send()
            first_info(k, delta).wait_send()
            for to in range(2):
                late(k, delta, to).wait_send()

    for k in range(3):
        for way in range(2):
            far(k, way).wait_send()
            for part in range(2):
                near(k, 1 + 2 * way, part).wait_send()

    @pl.loop(0, 2)
    def _(q):
        for k in range(3):
            beside(q, k).wait_send()
            across(q, k).wait_send()
            for delta in DELTAS:
                forth(q, k, delta).wait_send()
                for o in range(2):
                    back(q, o, k, delta).wait_send()


def solution(mesh):
    group_axes = ("node", "expert")
    group_size = mesh.shape["node"] * mesh.shape["expert"]
    tok_spec = P(("data", "node", "expert"), None)
    weight_spec = P(("node", "expert"), None, None)
    hbm = pl.BlockSpec(memory_space=pltpu.HBM)
    vmem = pl.BlockSpec(memory_space=pltpu.VMEM)
    dma = pltpu.SemaphoreType.DMA

    def local_layer(tokens, expert_ids, gate_weights, slot_ids, w_gate, w_up, w_down):
        rows, width = tokens.shape
        top_k = expert_ids.shape[1]
        slots = capacity(rows, top_k, group_size)
        bf = jnp.bfloat16
        pos = jnp.where(slot_ids >= 0, expert_ids * slots + slot_ids, -1).astype(jnp.float32)
        meta = jnp.concatenate([pos.T, gate_weights.T], axis=0)
        f32 = jnp.float32
        own, came = pl.pallas_call(
            lambda *refs: layer_kernel(slots, *refs),
            name="layer",
            in_specs=[vmem, vmem, hbm, hbm, hbm],
            out_specs=[hbm] * 5,
            out_shape=[
                jax.ShapeDtypeStruct((4, 2, 4, 4, slots, width), bf), jax.ShapeDtypeStruct((2, 4, 2, 4, 4, slots // 2, width), bf),
                jax.ShapeDtypeStruct((4, 4, 2, 4, slots, width), bf), jax.ShapeDtypeStruct((rows, width), f32), jax.ShapeDtypeStruct((2, rows, width), f32),
            ],
            scratch_shapes=[pltpu.VMEM((3, 4, 4, 16, rows), f32), pltpu.VMEM((4, 4, rows, width), bf)] + [pltpu.VMEM((2, 4, 2, slots, n), bf) for _, n in COLS]
            + [pltpu.VMEM((2, 2, 4, 4, 4, slots // 2, width), bf), pltpu.VMEM((2, 4, 2, 4, slots // 2, width), bf)]
            + [pltpu.VMEM(w.shape[1:], bf) for w in (w_gate, w_up, w_down)]
            + [pltpu.VMEM((4, rows, width), f32), pltpu.VMEM((2, rows // 2, width), f32)]
            + [dma((2, 3)), dma((3, 2))] + [dma((3, 3))] * 4 + [dma((3, 4, 2))] * 2 + [dma((3, 4, 3))] * 2 + [dma((3, 4, 2))] * 2
            + [dma((3,)), dma((4, 2, 3))] + [dma((3, 4, 4, 2))] * 2 + [dma((2, 3, 4, 2))] * 4 + [dma((2, 3, 3))] * 2
            + [dma((3, 2))] * 2 + [dma((2, 4, 3, 2))] + [dma((3, 2))] * 2 + [dma((3, 2, 2))] * 2,
            compiler_params=pltpu.CompilerParams(collective_id=1, has_side_effects=True, vmem_limit_bytes=67043328),
        )(tokens, meta, w_gate, w_up, w_down)[3:]
        return (own + (came[0] + came[1])).astype(bf)

    return jax.shard_map(local_layer, mesh=mesh, in_specs=(tok_spec, tok_spec, tok_spec, tok_spec, weight_spec, weight_spec, weight_spec), out_specs=tok_spec, check_vma=False)
```

time: 322 us -> 308 us (0.957)
  Pallas kernels: 317 us -> 302 us
  other arithmetic: 2.02 us -> 6.29 us
    pallas_call x3 -> x1, Pallas kernels: 317 us -> 302 us  [local_layer(): pl.pallas_call(lambda *refs: layer_kernel(slots, *refs), name='layer', in...]
    convert_element_type x0 -> x1, other arithmetic: none -> 4.27 us  [local_layer(): return (own + (came[0] + came[1])).astype(bf)]
where the time goes in v4:
time: 308 us
  Pallas kernels  302 us (98%)
  other arithmetic  6.29 us (2%)
    pallas_call x1, Pallas kernels, local_layer(): pl.pallas_call(lambda *refs: layer_kernel(slots, *refs), name='layer', in...  302 us

profile of v4, /device:TPU:1, one launch (start us, length us, event | category | flops | bytes accessed | tf_op | source)
XLA Modules:
  0.0 307.9 jit_solution(6023043279317352320)
XLA Ops:
  0.0 0.7 convert_bitcast_fusion
  0.7 1.3 pad_maximum_fusion.refs_1_
  2.0 301.6 %layer.1 = (bf16[4,2,4,4,32,2048]{5,4,3,2,1,0:T(8,128)(2,1)}, bf16[2,4,2,4,4,16,2048]{6,5,4,3,2,1,0:T(8,128)(2,1)}, bf16[4,4,2,4,32,2048]{5,4,3,2,1,0:T(8,128)(2,1)}, f32[256,2048]{1,0:T(8,128)}, f32[2,256,2048]{2,1,0:T(8,128)}) custom-call(bf16[256,2048]{1,0:T(8,128)(2,1)} %refs_0_.1, f32[16,256]{1,0:T(8,128)} %pad_maximum_fusion.refs_1_, ...), custom_call_target="tpu_custom_call" | custom-call | tf_op jit(solution)/shard_map/layer/pallas_call | solution.py:526
  303.6 4.3 %fusion = bf16[256,2048]{1,0:T(8,128)(2,1)} fusion(f32[256,2048]{1,0:T(8,128)} %get-tuple-element.7, f32[2,256,2048]{2,1,0:T(8,128)} %get-tuple-element.8), kind=kLoop, calls=%fused_computation.1 | loop fusion | flops 1572864 | bytes 7340032 | tf_op jit(solution)/shard_map/convert_element_type | solution.py:544

commit v5 on v4

--- a/solution.py
+++ b/solution.py
@@ -373,8 +373,16 @@
         for way in range(2):
             relay(k, way).wait_send()
 
+    @pl.loop(0, 2)
+    def _(q):
+        for k in range(3):
+            across(q, k).wait_send()
+            for delta in DELTAS:
+                for o in range(2):
+                    back(q, o, k, delta).wait_send()
+
     def fetch(q, turn, k, c):
-        d0 = lax.rem(v[dims(k)[0]] + RING - turn + 2, RING)
+        d0 = lax.rem(v[dims(k)[0]] + turn_delta(turn), RING)
         return pltpu.make_async_copy(z5.at[:, :, c, d0, span(q), cols(k)], t2.at[:, :, pl.ds(32 * (RING * q + turn) + half_slots * c, half_slots), cols(k)], load_sem.at[q, turn, k, c])
 
     def near(k, delta, part):
@@ -399,11 +407,13 @@
     lane = lax.broadcasted_iota(jnp.int32, (1, n), 1)
     place_of = (lane // (RING * 2 * half_slots), (lane // (2 * half_slots)) % RING, (lane // half_slots) % 2, lane % half_slots)
 
-    def weigh(q, turn, delta, k):
+    def turn_delta(turn):
+        h = turn // 2
+        return (1 - h) * (2 - turn) + h * (9 - 3 * turn)
+
+    def weights(q, delta, k):
         d1, p2, half, s = place_of
         i0, i1, i2 = dims(k)
-        for c in range(2):
-            fetch(q, turn, k, c).wait()
         a, b = at(k, delta, 0)
         m = jnp.transpose(mt[k, a, b])
         key = ((half * 64 + v[i0] * st[i0] + d1 * st[i1] + p2 * st[i2]) * slots + half_slots * q + s).astype(jnp.float32)
@@ -414,35 +424,42 @@
         rest = w - hi.astype(jnp.float32)
         mid = rest.astype(jnp.bfloat16)
         low = (rest - mid.astype(jnp.float32)).astype(jnp.bfloat16)
+        return low, mid, hi
+
+    def weigh(q, turn, k, terms):
+        for c in range(2):
+            fetch(q, turn, k, c).wait()
         y = t2[:, :, pl.ds(32 * (RING * q + turn), 32), cols(k)].reshape(n, COLS[k][1])
-        total = jnp.dot(low, y, preferred_element_type=jnp.float32)
-        total += jnp.dot(mid, y, preferred_element_type=jnp.float32)
-        total += jnp.dot(hi, y, preferred_element_type=jnp.float32)
-        if q == 0:
-            sums[delta, :, cols(k)] = total
-        else:
-            sums[delta, :, cols(k)] += total
-
-    def turn_delta(turn):
-        return lax.rem(RING - turn + 2, RING)
+        got = jnp.dot(jnp.concatenate(terms, axis=0), y, preferred_element_type=jnp.float32)
+        return (got[:rows] + got[rows:2 * rows]) + got[2 * rows:]
+
+    @pl.loop(0, RING)
+    def _(turn):
+        for k in range(3):
+            for i, term in enumerate(weights(1, turn_delta(turn), k)):
+                r[k // 2, k % 2, turn, :, :, :, pl.ds(n * i, n)] = term.reshape(RING, RING, half_slots, n)
 
     for q in range(2):
         for k in range(3):
-            lift(q, k, 1).wait()
             i1 = dims(k)[1]
             for delta in DELTAS:
                 target = z5.at[lax.rem(v[i1] + 4 - delta, RING), :, :, :, span(q), cols(k)]
                 remote(target, target, s5.at[q, k, delta - 1], r5.at[q, k, delta - 1], core, e).wait_recv()
+            lift(q, k, 1).wait()
             for turn in range(RING):
                 for c in range(2):
                     fetch(q, turn, k, c).start()
 
         @pl.loop(0, RING)
         def _(turn):
+            delta = turn_delta(turn)
             for k in range(3):
-                delta = turn_delta(turn)
-                weigh(q, turn, delta, k)
-                if q == 1:
+                if q == 0:
+                    sums[delta, :, cols(k)] = weigh(q, turn, k, weights(q, delta, k))
+                else:
+                    terms = [r[k // 2, k % 2, turn, :, :, :, pl.ds(n * i, n)].reshape(rows, n) for i in range(3)]
+                    sums[delta, :, cols(k)] += weigh(q, turn, k, terms)
+
                     @pl.when(turn == 0)
                     def _():
                         for way in range(2):
@@ -452,16 +469,12 @@
                     def _():
                         near(k, 1, 1).start()
 
-                    @pl.when(turn == 3)
+                    @pl.when(turn == 2)
                     def _():
                         near(k, 3, 0).start()
 
-            if q == 1:
-                @pl.when(turn == 2)
-                def _():
-                    for k in range(3):
-                        join(k, 1)
-
+    for k in range(3):
+        join(k, 1)
     for k in range(3):
         join(k, 3)
     keep = pltpu.make_async_copy(sums.at[0], own, load_sem.at[0, 0, 0, 0])
@@ -499,11 +512,8 @@
     def _(q):
         for k in range(3):
             beside(q, k).wait_send()
-            across(q, k).wait_send()
             for delta in DELTAS:
                 forth(q, k, delta).wait_send()
-                for o in range(2):
-                    back(q, o, k, delta).wait_send()
 
 
 def solution(mesh):

time: 308 us -> 299 us (0.971)
  Pallas kernels: 302 us -> 292 us
    pallas_call x1, Pallas kernels: 302 us -> 292 us  [local_layer(): pl.pallas_call(lambda *refs: layer_kernel(slots, *refs), name='layer', in...]
where the time goes in v5:
time: 299 us; the launch traced here: 298 us
  Pallas kernels  292 us (98%)
  other arithmetic  6.29 us (2%)
    pallas_call x1, Pallas kernels, local_layer(): pl.pallas_call(lambda *refs: layer_kernel(slots, *refs), name='layer', in...  292 us

profile of v5, /device:TPU:1, one launch (start us, length us, event | category | flops | bytes accessed | tf_op | source)
XLA Modules:
  0.0 298.2 jit_solution(12048230834037419989)
XLA Ops:
  0.0 0.7 convert_bitcast_fusion
  0.7 1.3 pad_maximum_fusion.refs_1_
  2.0 291.9 %layer.1 = (bf16[4,2,4,4,32,2048]{5,4,3,2,1,0:T(8,128)(2,1)}, bf16[2,4,2,4,4,16,2048]{6,5,4,3,2,1,0:T(8,128)(2,1)}, bf16[4,4,2,4,32,2048]{5,4,3,2,1,0:T(8,128)(2,1)}, f32[256,2048]{1,0:T(8,128)}, f32[2,256,2048]{2,1,0:T(8,128)}) custom-call(bf16[256,2048]{1,0:T(8,128)(2,1)} %refs_0_.1, f32[16,256]{1,0:T(8,128)} %pad_maximum_fusion.refs_1_, ...), custom_call_target="tpu_custom_call" | custom-call | tf_op jit(solution)/shard_map/layer/pallas_call | solution.py:536
  293.9 4.3 %fusion = bf16[256,2048]{1,0:T(8,128)(2,1)} fusion(f32[256,2048]{1,0:T(8,128)} %get-tuple-element.7, f32[2,256,2048]{2,1,0:T(8,128)} %get-tuple-element.8), kind=kLoop, calls=%fused_computation.1 | loop fusion | flops 1572864 | bytes 7340032 | tf_op jit(solution)/shard_map/convert_element_type | solution.py:554

commit v6 on v5

--- a/solution.py
+++ b/solution.py
@@ -71,14 +71,16 @@
     return out
 
 
-def layer_kernel(slots, tok, meta, wg_ref, wu_ref, wd_ref, s_ref, z4, z5, own, came2, mt, t2, tile0, tile1, tile2, r, bounce, wg, wu, wd, sums, passing,
+def layer_kernel(slots, tok, where, gates, wg_ref, wu_ref, wd_ref, s_ref, z4, z5, own, came2, mt, t2, tile0, tile1, tile2, r, bounce, wg, wu, wd, sums, passing,
                  loc0, out_sem, s1s, s1r, m1s, m1r, s2s, s2r, m2s, m2r, s3s, s3r, wsem, loc, xes, xer, xs, xr, s4, r4, s5, r5,
-                 relay_s, relay_r, load_sem, hs, hr, ps, pr):
+                 relay_s, relay_r, load_sem, hs, hr, ps, pr, s6, r6, meta):
     core, e, views = place()
     v, st = own_view(core, views)
     other = own_view(1 - core, views)[0]
     half_slots = slots // 2
     loads = [pltpu.make_async_copy(src.at[0], dst, wsem.at[i]) for i, (src, dst) in enumerate(((wg_ref, wg), (wu_ref, wu), (wd_ref, wd)))]
+    meta[:8] = where[...]
+    meta[8:] = gates[...]
     greet(ring_peers((0, 1), e, views) + [(1 - core, e)])
     rows = tok.shape[0]
     tiles = (tile0, tile1, tile2)
@@ -339,6 +341,20 @@
         i1 = dims(k)[1]
         return remote(line(q, k, lax.rem(v[i1] + delta, RING)), z5.at[v[i1], :, :, :, span(q), cols(k)], s5.at[q, k, delta - 1], r5.at[q, k, delta - 1], core, step(e, v[i1], st[i1], delta))
 
+    def turn_delta(turn):
+        h = turn // 2
+        return (1 - h) * (2 - turn) + h * (9 - 3 * turn)
+
+    def column(turn, k, from_d1):
+        d0 = lax.rem(v[dims(k)[0]] + turn_delta(turn), RING)
+        return z5.at[from_d1, :, :, d0, span(1), cols(k)]
+
+    def single(turn, k, delta):
+        i0, i1, _ = dims(k)
+        d0, d1 = lax.rem(v[i0] + turn_delta(turn), RING), lax.rem(v[i1] + delta, RING)
+        src = z4.at[(1, slice(None), slice(None), *plane_at(k, d0, d1), slice(None), cols(k))]
+        return remote(src, column(turn, k, v[i1]), s6.at[k, turn, delta - 1], r6.at[k, turn, delta - 1], core, step(e, v[i1], st[i1], delta))
+
     def lift(q, k, stage):
         i1 = dims(k)[1]
         room = bounce.at[q, :, :, :, :, cols(k)]
@@ -356,9 +372,17 @@
                 for o in range(2):
                     target = z4_at(q, k, lax.rem(v[i2] + 4 - delta, RING), o)
                     remote(target, target, s4.at[q, k, delta, 0], r4.at[q, k, delta, o], core, e).wait_recv()
-            for delta in DELTAS:
-                forth(q, k, delta).start()
+            if q == 0:
+                for delta in DELTAS:
+                    forth(q, k, delta).start()
             lift(q, k, 0).start()
+        if q == 1:
+            @pl.loop(0, RING)
+            def _(turn):
+                for k in range(3):
+                    for delta in DELTAS:
+                        single(turn, k, delta).start()
+
         for k in range(3):
             lift(q, k, 0).wait()
             lift(q, k, 1).start()
@@ -406,10 +430,6 @@
     n = RING * RING * 2 * half_slots
     lane = lax.broadcasted_iota(jnp.int32, (1, n), 1)
     place_of = (lane // (RING * 2 * half_slots), (lane // (2 * half_slots)) % RING, (lane // half_slots) % 2, lane % half_slots)
-
-    def turn_delta(turn):
-        h = turn // 2
-        return (1 - h) * (2 - turn) + h * (9 - 3 * turn)
 
     def weights(q, delta, k):
         d1, p2, half, s = place_of
@@ -441,18 +461,28 @@
 
     for q in range(2):
         for k in range(3):
-            i1 = dims(k)[1]
-            for delta in DELTAS:
-                target = z5.at[lax.rem(v[i1] + 4 - delta, RING), :, :, :, span(q), cols(k)]
-                remote(target, target, s5.at[q, k, delta - 1], r5.at[q, k, delta - 1], core, e).wait_recv()
             lift(q, k, 1).wait()
-            for turn in range(RING):
-                for c in range(2):
-                    fetch(q, turn, k, c).start()
+        if q == 0:
+            for k in range(3):
+                i1 = dims(k)[1]
+                for delta in DELTAS:
+                    target = z5.at[lax.rem(v[i1] + 4 - delta, RING), :, :, :, span(0), cols(k)]
+                    remote(target, target, s5.at[0, k, delta - 1], r5.at[0, k, delta - 1], core, e).wait_recv()
+                for turn in range(RING):
+                    for c in range(2):
+                        fetch(0, turn, k, c).start()
 
         @pl.loop(0, RING)
         def _(turn):
             delta = turn_delta(turn)
+            if q == 1:
+                for k in range(3):
+                    i1 = dims(k)[1]
+                    for d in DELTAS:
+                        target = column(turn, k, lax.rem(v[i1] + 4 - d, RING))
+                        remote(target, target, s6.at[k, turn, d - 1], r6.at[k, turn, d - 1], core, e).wait_recv()
+                    for c in range(2):
+                        fetch(1, turn, k, c).start()
             for k in range(3):
                 if q == 0:
                     sums[delta, :, cols(k)] = weigh(q, turn, k, weights(q, delta, k))
@@ -490,6 +520,7 @@
     def _(j):
         for k in range(3):
             for delta in DELTAS:
+                single(j, k, delta).wait_send()
                 second_info(k, j, delta).wait_send()
                 for to in range(2):
                     early(k, j, delta, to).wait_send()
@@ -499,6 +530,7 @@
             if delta != 2:
                 first(k, delta).wait_send()
             first_info(k, delta).wait_send()
+            forth(0, k, delta).wait_send()
             for to in range(2):
                 late(k, delta, to).wait_send()
 
@@ -512,8 +544,6 @@
     def _(q):
         for k in range(3):
             beside(q, k).wait_send()
-            for delta in DELTAS:
-                forth(q, k, delta).wait_send()
 
 
 def solution(mesh):
@@ -531,12 +561,11 @@
         slots = capacity(rows, top_k, group_size)
         bf = jnp.bfloat16
         pos = jnp.where(slot_ids >= 0, expert_ids * slots + slot_ids, -1).astype(jnp.float32)
-        meta = jnp.concatenate([pos.T, gate_weights.T], axis=0)
         f32 = jnp.float32
         own, came = pl.pallas_call(
             lambda *refs: layer_kernel(slots, *refs),
             name="layer",
-            in_specs=[vmem, vmem, hbm, hbm, hbm],
+            in_specs=[vmem, vmem, vmem, hbm, hbm, hbm],
             out_specs=[hbm] * 5,
             out_shape=[
                 jax.ShapeDtypeStruct((4, 2, 4, 4, slots, width), bf), jax.ShapeDtypeStruct((2, 4, 2, 4, 4, slots // 2, width), bf),
@@ -548,9 +577,10 @@
             + [pltpu.VMEM((4, rows, width), f32), pltpu.VMEM((2, rows // 2, width), f32)]
             + [dma((2, 3)), dma((3, 2))] + [dma((3, 3))] * 4 + [dma((3, 4, 2))] * 2 + [dma((3, 4, 3))] * 2 + [dma((3, 4, 2))] * 2
             + [dma((3,)), dma((4, 2, 3))] + [dma((3, 4, 4, 2))] * 2 + [dma((2, 3, 4, 2))] * 4 + [dma((2, 3, 3))] * 2
-            + [dma((3, 2))] * 2 + [dma((2, 4, 3, 2))] + [dma((3, 2))] * 2 + [dma((3, 2, 2))] * 2,
+            + [dma((3, 2))] * 2 + [dma((2, 4, 3, 2))] + [dma((3, 2))] * 2 + [dma((3, 2, 2))] * 2
+            + [dma((3, 4, 3))] * 2 + [pltpu.VMEM((16, rows), f32)],
             compiler_params=pltpu.CompilerParams(collective_id=1, has_side_effects=True, vmem_limit_bytes=67043328),
-        )(tokens, meta, w_gate, w_up, w_down)[3:]
+        )(tokens, pos.T, gate_weights.T, w_gate, w_up, w_down)[3:]
         return (own + (came[0] + came[1])).astype(bf)
 
     return jax.shard_map(local_layer, mesh=mesh, in_specs=(tok_spec, tok_spec, tok_spec, tok_spec, weight_spec, weight_spec, weight_spec), out_specs=tok_spec, check_vma=False)

time: 299 us -> 291 us (0.973)
  Pallas kernels: 292 us -> 285 us
    pallas_call x1, Pallas kernels: 292 us -> 285 us  [local_layer(): pl.pallas_call(lambda *refs: layer_kernel(slots, *refs), name='layer', in...]
where the time goes in v6:
time: 291 us; the launch traced here: 290 us
  Pallas kernels  285 us (98%)
  other arithmetic  5.58 us (2%)
    pallas_call x1, Pallas kernels, local_layer(): pl.pallas_call(lambda *refs: layer_kernel(slots, *refs), name='layer', in...  285 us

profile of v6, /device:TPU:1, one launch (start us, length us, event | category | flops | bytes accessed | tf_op | source)
XLA Modules:
  0.0 290.2 jit_solution(15601866265014760197)
XLA Ops:
  0.0 1.3 convert_bitcast_fusion.refs_1_
  1.3 284.6 %layer.1 = (bf16[4,2,4,4,32,2048]{5,4,3,2,1,0:T(8,128)(2,1)}, bf16[2,4,2,4,4,16,2048]{6,5,4,3,2,1,0:T(8,128)(2,1)}, bf16[4,4,2,4,32,2048]{5,4,3,2,1,0:T(8,128)(2,1)}, f32[256,2048]{1,0:T(8,128)}, f32[2,256,2048]{2,1,0:T(8,128)}) custom-call(bf16[256,2048]{1,0:T(8,128)(2,1)} %refs_0_.1, f32[8,256]{1,0:T(8,128)} %convert_bitcast_fusion.refs_1_, ...), custom_call_target="tpu_custom_call" | custom-call | tf_op jit(solution)/shard_map/layer/pallas_call | solution.py:565
  285.9 4.3 %fusion = bf16[256,2048]{1,0:T(8,128)(2,1)} fusion(f32[256,2048]{1,0:T(8,128)} %get-tuple-element.7, f32[2,256,2048]{2,1,0:T(8,128)} %get-tuple-element.8), kind=kLoop, calls=%fused_computation.1 | loop fusion | flops 1572864 | bytes 7340032 | tf_op jit(solution)/shard_map/convert_element_type | solution.py:584

commit v7 on v6

--- a/solution.py
+++ b/solution.py
@@ -71,7 +71,7 @@
     return out
 
 
-def layer_kernel(slots, tok, where, gates, wg_ref, wu_ref, wd_ref, s_ref, z4, z5, own, came2, mt, t2, tile0, tile1, tile2, r, bounce, wg, wu, wd, sums, passing,
+def layer_kernel(slots, tok, ids, slot_of, gates, wg_ref, wu_ref, wd_ref, s_ref, z4, z5, own, came2, mt, t2, tile0, tile1, tile2, r, bounce, wg, wu, wd, sums, passing,
                  loc0, out_sem, s1s, s1r, m1s, m1r, s2s, s2r, m2s, m2r, s3s, s3r, wsem, loc, xes, xer, xs, xr, s4, r4, s5, r5,
                  relay_s, relay_r, load_sem, hs, hr, ps, pr, s6, r6, meta):
     core, e, views = place()
@@ -79,7 +79,7 @@
     other = own_view(1 - core, views)[0]
     half_slots = slots // 2
     loads = [pltpu.make_async_copy(src.at[0], dst, wsem.at[i]) for i, (src, dst) in enumerate(((wg_ref, wg), (wu_ref, wu), (wd_ref, wd)))]
-    meta[:8] = where[...]
+    meta[:8] = jnp.where(slot_of[...] >= 0, ids[...] * slots + slot_of[...], -1).astype(jnp.float32)
     meta[8:] = gates[...]
     greet(ring_peers((0, 1), e, views) + [(1 - core, e)])
     rows = tok.shape[0]
@@ -560,12 +560,11 @@
         top_k = expert_ids.shape[1]
         slots = capacity(rows, top_k, group_size)
         bf = jnp.bfloat16
-        pos = jnp.where(slot_ids >= 0, expert_ids * slots + slot_ids, -1).astype(jnp.float32)
         f32 = jnp.float32
         own, came = pl.pallas_call(
             lambda *refs: layer_kernel(slots, *refs),
             name="layer",
-            in_specs=[vmem, vmem, vmem, hbm, hbm, hbm],
+            in_specs=[vmem] * 4 + [hbm] * 3,
             out_specs=[hbm] * 5,
             out_shape=[
                 jax.ShapeDtypeStruct((4, 2, 4, 4, slots, width), bf), jax.ShapeDtypeStruct((2, 4, 2, 4, 4, slots // 2, width), bf),
@@ -580,7 +579,7 @@
             + [dma((3, 2))] * 2 + [dma((2, 4, 3, 2))] + [dma((3, 2))] * 2 + [dma((3, 2, 2))] * 2
             + [dma((3, 4, 3))] * 2 + [pltpu.VMEM((16, rows), f32)],
             compiler_params=pltpu.CompilerParams(collective_id=1, has_side_effects=True, vmem_limit_bytes=67043328),
-        )(tokens, pos.T, gate_weights.T, w_gate, w_up, w_down)[3:]
+        )(tokens, expert_ids.T, slot_ids.T, gate_weights.T, w_gate, w_up, w_down)[3:]
         return (own + (came[0] + came[1])).astype(bf)
 
     return jax.shard_map(local_layer, mesh=mesh, in_specs=(tok_spec, tok_spec, tok_spec, tok_spec, weight_spec, weight_spec, weight_spec), out_specs=tok_spec, check_vma=False)

time: 291 us -> 289 us (level)
  no operation moved by 1% of the time
where the time goes in v7:
time: 289 us
  Pallas kernels  285 us (99%)
  other arithmetic  4.27 us (1%)
    pallas_call x1, Pallas kernels, local_layer(): pl.pallas_call(lambda *refs: layer_kernel(slots, *refs), name='layer', in...  285 us

profile of v7, /device:TPU:1, one launch (start us, length us, event | category | flops | bytes accessed | tf_op | source)
XLA Modules:
  0.0 288.9 jit_solution(6856028271673504690)
XLA Ops:
  0.0 284.6 %layer.1 = (bf16[4,2,4,4,32,2048]{5,4,3,2,1,0:T(8,128)(2,1)}, bf16[2,4,2,4,4,16,2048]{6,5,4,3,2,1,0:T(8,128)(2,1)}, bf16[4,4,2,4,32,2048]{5,4,3,2,1,0:T(8,128)(2,1)}, f32[256,2048]{1,0:T(8,128)}, f32[2,256,2048]{2,1,0:T(8,128)}) custom-call(bf16[256,2048]{1,0:T(8,128)(2,1)} %refs_0_.1, s32[8,256]{1,0:T(8,128)} %bitcast.7, s32[8,256]{1,0:T(8,128)} %bitcast.8, ...), custom_call_target="tpu_custom_call" | custom-call | tf_op jit(solution)/shard_map/layer/pallas_call | solution.py:564
  284.6 4.3 %fusion = bf16[256,2048]{1,0:T(8,128)(2,1)} fusion(f32[256,2048]{1,0:T(8,128)} %get-tuple-element.7, f32[2,256,2048]{2,1,0:T(8,128)} %get-tuple-element.8), kind=kLoop, calls=%fused_computation.1 | loop fusion | flops 1572864 | bytes 7340032 | tf_op jit(solution)/shard_map/convert_element_type | solution.py:583
